TPU v7x, 512 devices: a 4x2x32 block of a 4x8x32 slice. The times are simulated.
512 devices in a mesh: groups: 2 (over y), tp: 8 (over x, core), sp: 32 (over z).
Axes of the slice: x: 4, y: 2, z: 32, core: 2. Of those that a mesh axis runs over, the one named last changes fastest.
The devices are a block of a 4x8x32 slice.
Arguments:
- query_rows: bfloat16 [4, 2048, 4096], P('groups', ('sp', 'tp')), parts along dimension 0, may hold values from -100 to 100
- key_rows: bfloat16 [4, 2048, 4096], P('groups', ('sp', 'tp')), parts along dimension 0, may hold values from -4 to 4
- value_rows: bfloat16 [4, 2048, 4096], P('groups', ('sp', 'tp')), parts along dimension 0, may hold values from -6 to 6
- residual: bfloat16 [4, 2048, 2560], P('groups', 'sp', 'tp'), parts along dimension 0, may hold values from -100 to 100
- modulation: float32 [4, 2560], P(None, 'tp'), may hold values from -3 to 3
- out_weight: bfloat16 [2560, 4096], P('tp', 'sp'), may hold values from -0.375 to 0.375
- up_weight: bfloat16 [2560, 7168], P('sp', 'tp'), may hold values from -0.125 to 0.125
- down_weight: bfloat16 [2560, 7168], P('sp', 'tp'), may hold values from -0.0625 to 0.0625
Outputs:
- block_out: bfloat16 [4, 2048, 2560], P('groups', 'sp', 'tp'), parts along dimension 0
There are 2 independent parts, one for each index of `groups`. A program takes and returns all parts, laid end to end along the dimension named above; an argument that names none is the same for every part. Nothing has to cross between parts.
All inputs are finite; a program needn't handle non-finite values.
Results may differ from a plain program's by a relative error of at most 0.0044.
Values may be sent and summed in bfloat16 or wider, within the bound.
No kernel may reach another device: no remote copies, remote signals or barrier semaphores. Data moves between devices by JAX's collectives and lax.ppermute only.
A program may use at most 64 MiB of HBM per device.

v0:
```python
import math

import jax
import jax.numpy as jnp
from jax import lax
from jax.sharding import PartitionSpec as P

D = 2560
HEAD_FEATURES = 128


def in_one_piece(arrays, axis, split_dim, concat_dim, along):
    widths = [a.shape[along] for a in arrays]
    both = jnp.concatenate(arrays, axis=along)
    filled = lax.all_to_all(both, axis, split_axis=split_dim, concat_axis=concat_dim, tiled=True)
    return tuple(jnp.split(filled, [sum(widths[:k]) for k in range(1, len(widths))], axis=along))


def side_by_side(arrays, axis, dim, along):
    both = jnp.concatenate(arrays, axis=along)
    filled, at, outs = (lax.all_gather(both, axis, axis=dim, tiled=True), 0, [])
    for a in arrays:
        outs.append(lax.slice_in_dim(filled, at, at + a.shape[along], axis=along))
        at += a.shape[along]
    return tuple(outs)


def sent_to_all(array, axis):
    copies = jnp.broadcast_to(array, (lax.axis_size(axis), *array.shape))
    return lax.all_to_all(copies, axis, split_axis=0, concat_axis=0, tiled=True)


def joined_along(parts, dim):
    dims = list(parts.shape[1:])
    dims[dim] *= parts.shape[0]
    return jnp.moveaxis(parts, 0, dim).reshape(dims)


def gathered_copies(array, axis, dim):
    parts = sent_to_all(array, axis)
    return joined_along(parts, dim)


def taken_together(array, axis):
    everything = sent_to_all(array, axis)
    return jnp.sum(everything, axis=0)


def packed_total(arrays, axis):
    flat, at, outs = (jnp.concatenate([a.reshape(-1) for a in arrays]), 0, [])
    so_far = taken_together(flat, axis)
    for a in arrays:
        outs.append(so_far[at : at + a.size].reshape(a.shape))
        at += a.size
    return tuple(outs)


def in_blocks(array, dim, peers):
    before, after = (array.shape[:dim], array.shape[dim + 1 :])
    return jnp.moveaxis(array.reshape(*before, peers, -1, *after), dim, 0)


def sent_and_summed(array, axis, dim):
    peers = lax.axis_size(axis)
    parts = lax.all_to_all(in_blocks(array, dim, peers), axis, 0, 0, tiled=True)
    return jnp.sum(parts.astype(jnp.float32), axis=0)


def contract_last(left, right):
    return lax.dot_general(
        left, right, (((1,), (1,)), ((), ())), preferred_element_type=jnp.float32
    )


def attend(query_part, key_part, value_part):
    query_heads, key_heads, value_heads = in_one_piece(
        (query_part, key_part, value_part), "sp", 2, 1, 0
    )
    batches, query_count, local_width = query_heads.shape
    local_heads = local_width // HEAD_FEATURES
    grouped = query_heads.reshape(batches, query_count, local_heads, HEAD_FEATURES)
    score_scale = 1.0 / math.sqrt(HEAD_FEATURES)

    def absorb_block(running, blocks):
        block_keys, block_values = blocks
        highest, row_total, weighted_values = running
        attention_logits = (
            jnp.einsum("bqhd,bkhd->bqhk", grouped, block_keys, preferred_element_type=jnp.float32)
            * score_scale
        )
        raised = jnp.maximum(highest, jnp.max(attention_logits, axis=-1))
        damping = jnp.exp(highest - raised)
        exponent = jnp.exp(attention_logits - raised[..., None])
        row_total = row_total * damping + jnp.sum(exponent, axis=-1)
        weighted_values = weighted_values * damping[..., None] + jnp.einsum(
            "bqhk,bkhd->bqhd",
            exponent.astype(jnp.bfloat16),
            block_values,
            preferred_element_type=jnp.float32,
        )
        return (raised, row_total, weighted_values)

    def scan_step(running, blocks):
        return (absorb_block(running, blocks), None)

    starting = (
        jnp.full((batches, query_count, local_heads), -jnp.inf, jnp.float32),
        jnp.zeros((batches, query_count, local_heads), jnp.float32),
        jnp.zeros((batches, query_count, local_heads, HEAD_FEATURES), jnp.float32),
    )
    running = starting
    key_section, value_section = side_by_side((key_heads, value_heads), "tp", 1, 0)
    key_count = key_section.shape[1]
    shaped_keys = key_section.reshape(batches, key_count, local_heads, HEAD_FEATURES)
    shaped_values = value_section.reshape(batches, key_count, local_heads, HEAD_FEATURES)
    block_count = key_count // 512
    key_blocks = jnp.moveaxis(
        shaped_keys.reshape(batches, block_count, 512, local_heads, HEAD_FEATURES), 1, 0
    )
    value_blocks = jnp.moveaxis(
        shaped_values.reshape(batches, block_count, 512, local_heads, HEAD_FEATURES), 1, 0
    )
    running, unused = lax.scan(scan_step, running, (key_blocks, value_blocks))
    highest, row_total, weighted_values = running
    normalized = (weighted_values / row_total[..., None]).astype(jnp.bfloat16)
    ordered = normalized.reshape(batches, query_count, local_width)
    return lax.all_to_all(ordered, "sp", split_axis=1, concat_axis=2, tiled=True)


def body(
    query_rows, key_rows, value_rows, residual, modulation, out_weight, up_weight, down_weight
):
    attended = attend(query_rows, key_rows, value_rows)
    stripes = gathered_copies(attended, "tp", 1)
    batches, rows_block, inner_width = stripes.shape
    row_count = batches * rows_block
    flat_rows = stripes.reshape(row_count, inner_width)
    local_width = out_weight.shape[0]
    columns = flat_rows
    projected = contract_last(columns, lax.all_gather(out_weight, "sp", axis=1, tiled=True))
    mixed_rows = (
        residual.reshape(row_count, local_width).astype(jnp.float32) + modulation[0] * projected
    )
    first_sum, second_sum = packed_total(
        (jnp.sum(mixed_rows, axis=1), jnp.sum(mixed_rows * mixed_rows, axis=1)), "tp"
    )
    row_mean = first_sum / D
    spread = second_sum / D - row_mean * row_mean
    normed = (
        (mixed_rows - row_mean[:, None])
        * lax.rsqrt(spread[:, None] + 1e-06)
        * (1.0 + modulation[2])
        + modulation[1]
    ).astype(jnp.bfloat16)
    gathered = gathered_copies(normed, "tp", 1)
    columns = gathered
    hidden = jnp.dot(
        columns,
        lax.all_gather(up_weight, "sp", axis=0, tiled=True),
        preferred_element_type=jnp.float32,
    )
    active = jax.nn.gelu(hidden, approximate=True).astype(jnp.bfloat16)
    partial_out = contract_last(active, lax.all_gather(down_weight, "sp", axis=0, tiled=True))
    summed = sent_and_summed(partial_out.astype(jnp.bfloat16), "tp", 1)
    result = (mixed_rows + modulation[3] * summed).astype(jnp.bfloat16)
    return result.reshape(batches, rows_block, local_width)


def solution(mesh):
    in_specs = (
        P("groups", ("sp", "tp"), None),
        P("groups", ("sp", "tp"), None),
        P("groups", ("sp", "tp"), None),
        P("groups", "sp", "tp"),
        P(None, "tp"),
        P("tp", "sp"),
        P("sp", "tp"),
        P("sp", "tp"),
    )
    out_specs = P("groups", "sp", "tp")
    return jax.shard_map(body, mesh=mesh, in_specs=in_specs, out_specs=out_specs, check_vma=False)
```

profile of v0, /device:TPU:33, one launch (start us, length us, event | category | flops | bytes accessed | tf_op | source)
XLA Modules:
  0.0 618.6 jit_solution(4592646324095410421)
XLA Ops:
  6.6 1.1 pad_maximum_fusion
  7.6 7.2 %copy.59 = bf16[6,8,4096]{1,0,2:T(8,128)(2,1)} copy(bf16[6,8,4096]{2,1,0:T(8,128)(2,1)S(1)} %pad_maximum_fusion) | data formatting | bytes 786432 | tf_op jit(solution)/shard_map/concatenate | solution.py:14
  14.8 9.2 %reshape.73 = bf16[32,2,3072]{2,1,0:T(2,128)(2,1)S(1)} reshape(bf16[4096,6,8]{2,1,0:T(8,128)(2,1)} %bitcast.97) | data formatting | bytes 786432
  24.0 97.4 %all_to_all.54 = bf16[32,2,3072]{2,1,0:T(2,128)(2,1)S(1)} all-to-all(bf16[32,2,3072]{2,1,0:T(2,128)(2,1)S(1)} %reshape.73), channel_id=1, replica_groups=mesh['groups'=2,'tp'=8,'sp'=32] {'sp'}, dimensions={0} | all-to-all | bytes 786432 | tf_op jit(solution)/shard_map/all_to_all | solution.py:15
  121.3 8.7 %reshape.74 = bf16[4096,6,8]{2,1,0:T(8,128)(2,1)} reshape(bf16[32,2,3072]{2,1,0:T(2,128)(2,1)S(1)} %all_to_all.54) | data formatting | bytes 786432
  130.0 7.4 %copy.60 = bf16[6,8,32,128]{3,1,2,0:T(8,128)(2,1)S(1)} copy(bf16[6,8,32,128]{1,0,3,2:T(8,128)(2,1)} %bitcast.98) | data formatting | bytes 786432 | tf_op jit(solution)/shard_map/all_to_all | solution.py:15
  137.5 0.7 pad_maximum_fusion.1
  138.3 0.7 all-gather.7.cloned.1.call-update
  139.1 0.7 all-gather.11.cloned.1.call-update
  139.9 0.6 all-gather.9.cloned.1.call-update
  140.5 24.1 %all-gather.5.cloned.1.call-done = bf16[4,2048,128]{2,1,0:T(8,128)(2,1)} async-done(((bf16[4,256,128]{2,1,0:T(8,128)(2,1)}), bf16[4,2048,128]{2,1,0:T(8,128)(2,1)}) %all-gather.5.cloned.1.call-update) | async-done | bytes 2097168 | tf_op jit(solution)/shard_map/all_gather | solution.py:21
  164.6 1.7 fusion.36
  166.3 3.9 while.15
  166.3 0.3 fusion.52
  166.7 0.4 fusion.55
  167.1 0.2 fusion.54
  167.3 0.3 fusion.52
  167.6 0.4 fusion.55
  168.1 0.2 fusion.54
  168.3 0.3 fusion.52
  168.6 0.4 fusion.55
  169.0 0.2 fusion.54
  169.2 0.3 fusion.52
  169.6 0.4 fusion.55
  170.0 0.2 fusion.54
  170.2 0.1 copy.64
  170.4 0.1 copy.63
  170.5 0.3 fusion.29
  170.9 53.5 %all_to_all.55 = bf16[2,256,128]{2,0,1:T(2,128)(2,1)S(1)} all-to-all(bf16[2,256,128]{2,0,1:T(2,128)(2,1)S(1)} %fusion.29), channel_id=1, replica_groups=mesh['groups'=2,'tp'=8,'sp'=32] {'sp'}, dimensions={1} | all-to-all | bytes 262144 | tf_op jit(solution)/shard_map/all_to_all | solution.py:127
  224.4 1.1 broadcast_in_dim.27
  225.5 6.0 all-to-all-start.2
  231.5 0.1 copy.67
  231.7 14.9 %all-to-all-done.2 = bf16[8,2,8,4096]{3,2,1,0:T(8,128)(2,1)S(1)} async-done(((bf16[8,2,8,4096]{3,2,1,0:T(8,128)(2,1)}), bf16[8,2,8,4096]{3,2,1,0:T(8,128)(2,1)S(1)}, u32[]{:S(2)}, u32[]{:S(2)}) %all-to-all-start.2) | async-done | bytes 1048608 | tf_op jit(solution)/shard_map/all_to_all | solution.py:30
  246.6 0.1 copy.66
  246.7 47.1 %all-gather.7.cloned.1.call-done = bf16[320,4096]{1,0:T(8,128)(2,1)} async-done(((bf16[320,128]{1,0:T(8,128)(2,1)}), bf16[320,4096]{1,0:T(8,128)(2,1)}) %all-gather.7.cloned.1.call-update) | async-done | bytes 2621456 | tf_op jit(solution)/shard_map/all_gather | solution.py:140
  293.8 2.6 fusion.34
  296.4 33.6 %all_to_all.56 = f32[8,1,256]{2,1,0:T(1,128)S(1)} all-to-all(f32[8,1,256]{2,1,0:T(1,128)S(1)} %broadcast_in_dim.28), channel_id=1, replica_groups=mesh['groups'=2,'tp'=8,'sp'=32] {'tp'}, dimensions={0} | all-to-all | bytes 16384 | tf_op jit(solution)/shard_map/all_to_all | solution.py:30
  330.1 0.2 add_convert_fusion.1
  330.3 0.9 broadcast_in_dim.29
  331.2 4.2 all-to-all-start.4
  335.4 99.1 %all-gather.11.cloned.1.call-done = bf16[2560,896]{1,0:T(8,128)(2,1)} async-done(((bf16[80,896]{1,0:T(8,128)(2,1)}), bf16[2560,896]{1,0:T(8,128)(2,1)}) %all-gather.11.cloned.1.call-update) | async-done | bytes 4587536 | tf_op jit(solution)/shard_map/all_gather | solution.py:163
  434.5 134.8 %all-gather.9.cloned.1.call-done = bf16[2560,896]{1,0:T(8,128)(2,1)} async-done(((bf16[80,896]{1,0:T(8,128)(2,1)}), bf16[2560,896]{1,0:T(8,128)(2,1)}) %all-gather.9.cloned.1.call-update) | async-done | bytes 4587536 | tf_op jit(solution)/shard_map/all_gather | solution.py:159
  569.3 6.0 convolution_convert_fusion
  575.3 0.3 copy.69
  575.7 35.5 %all_to_all.57 = bf16[8,128,320]{1,2,0:T(8,128)(2,1)S(1)} all-to-all(bf16[8,128,320]{1,2,0:T(8,128)(2,1)S(1)} %bitcast.103), channel_id=1, replica_groups=mesh['groups'=2,'tp'=8,'sp'=32] {'tp'}, dimensions={0} | all-to-all | bytes 1310720 | tf_op jit(solution)/shard_map/all_to_all | solution.py:65
  611.1 0.1 convert_reduce_fusion
  611.2 0.1 add_convert_fusion
  611.3 0.8 copy.70
  (33 shorter events, 0.5 us)
Async XLA Ops:
  6.5 158.1 %all-gather.5.cloned.1.call-start = ((), (), s32[]{:S(2)}) async-start(), calls=%async_computation.6 | async-start | bytes 2359296 | tf_op jit(solution)/shard_map/all_gather | solution.py:21
  138.2 155.6 %all-gather.7.cloned.1.call-start = ((), (), s32[]{:S(2)}) async-start(), calls=%async_computation.7 | async-start | bytes 2703360 | tf_op jit(solution)/shard_map/all_gather | solution.py:140
  139.1 295.4 %all-gather.11.cloned.1.call-start = ((), (), s32[]{:S(2)}) async-start(), calls=%async_computation.9 | async-start | bytes 4730880 | tf_op jit(solution)/shard_map/all_gather | solution.py:163
  139.9 429.4 %all-gather.9.cloned.1.call-start = ((), (), s32[]{:S(2)}) async-start(), calls=%async_computation.8 | async-start | bytes 4730880 | tf_op jit(solution)/shard_map/all_gather | solution.py:159
  170.2 61.3 %copy-start = (bf16[2,64,320]{2,1,0:T(8,128)(2,1)S(1)}, bf16[2,64,320]{2,1,0:T(8,128)(2,1)}, u32[]{:S(2)}) copy-start(bf16[2,64,320]{2,1,0:T(8,128)(2,1)} %param.13) | copy-start | bytes 245764
  170.2 61.4 %copy-start.1 = (f32[4,320]{1,0:T(4,128)S(1)}, f32[4,320]{1,0:T(4,128)}, u32[]{:S(2)}) copy-start(f32[4,320]{1,0:T(4,128)} %param.14) | copy-start | bytes 15364
  225.5 21.0 %all-to-all-start.2 = ((bf16[8,2,8,4096]{3,2,1,0:T(8,128)(2,1)}), bf16[8,2,8,4096]{3,2,1,0:T(8,128)(2,1)S(1)}, u32[]{:S(2)}, u32[]{:S(2)}) async-start(bf16[8,2,8,4096]{3,2,1,0:T(8,128)(2,1)} %broadcast_in_dim.27), calls=%async_computation.2 | async-start | bytes 2097152 | tf_op jit(solution)/shard_map/all_to_all | solution.py:30
  331.2 238.1 %all-to-all-start.4 = ((bf16[8,128,320]{1,2,0:T(8,128)(2,1)}), bf16[8,128,320]{1,2,0:T(8,128)(2,1)S(1)}, u32[]{:S(2)}, u32[]{:S(2)}) async-start(bf16[8,128,320]{1,2,0:T(8,128)(2,1)} %broadcast_in_dim.29), calls=%async_computation.4 | async-start | bytes 1310720 | tf_op jit(solution)/shard_map/all_to_all | solution.py:30
Sparse Core Ops, SparseCore 0:
  138.4 26.1 all-gather.4
  166.6 127.1 all-gather.6
  295.9 138.4 all-gather.10
  436.4 132.8 all-gather.8
where the time goes:
time: 619 us
  waiting for transfers between devices  322 us (52%)
  blocking collectives  220 us (36%)
  local copies, waits for them, and re-layouts  37.8 us (6%)
  between operations  13.3 us (2%)
  matrix products  11.6 us (2%)
  starting transfers between devices  10.3 us (2%)
    all_gather x1, waiting for transfers between devices, body(): lax.all_gather(up_weight, 'sp', axis=0, tiled=True)  135 us
    all_gather x1, waiting for transfers between devices, body(): lax.all_gather(down_weight, 'sp', axis=0, tiled=True)  99.1 us
    all_to_all x1, blocking collectives, in_one_piece(): lax.all_to_all(both, axis, split_axis=split_dim, concat_axis=concat_dim,...  97.4 us
    all_to_all x1, blocking collectives, attend(): lax.all_to_all(ordered, 'sp', split_axis=1, concat_axis=2, tiled=True)  53.5 us
    all_gather x1, waiting for transfers between devices, body(): lax.all_gather(out_weight, 'sp', axis=1, tiled=True)  47.1 us
    all_to_all x1, blocking collectives, sent_and_summed(): parts = lax.all_to_all(in_blocks(array, dim, peers), axis, 0, 0, tiled=True)  35.5 us
    all_to_all x1, blocking collectives, sent_to_all(): return lax.all_to_all(copies, axis, split_axis=0, concat_axis=0, tiled=True)  33.6 us
    all_gather x1, waiting for transfers between devices, side_by_side(): filled, at, outs = (lax.all_gather(both, axis, axis=dim, tiled=True), 0, [])  24.1 us
  transfers between devices with their start and end apart: 6, of which 5 were waited for; matrix products, arithmetic and copies ran while one was open for 2% of the time, Pallas kernels for 0%

commit v1 on v0

v1 whole, which is shorter than its diff:
```python
import math

import jax
import jax.numpy as jnp
from jax import lax
from jax.sharding import Mesh, PartitionSpec as P

D = 2560
HEAD_FEATURES = 128
LANES = 128
CORES = 2


def contract_last(left, right):
    return lax.dot_general(
        left, right, (((1,), (1,)), ((), ())), preferred_element_type=jnp.float32
    )


def sent_to_all(array, axis):
    copies = jnp.broadcast_to(array, (lax.axis_size(axis), *array.shape))
    return lax.all_to_all(copies, axis, split_axis=0, concat_axis=0, tiled=True)


def gathered_weights(out_weight, up_weight, down_weight):
    groups = lax.axis_size("groups")
    depth, units = up_weight.shape
    pieces = [
        out_weight,
        jnp.swapaxes(up_weight.reshape(depth, units // LANES, LANES), 0, 1).reshape(-1, LANES),
        jnp.swapaxes(down_weight.reshape(depth, units // LANES, LANES), 0, 1).reshape(-1, LANES),
    ]
    packed = jnp.concatenate(pieces, axis=0)
    rows = packed.shape[0]
    chunk = -(-rows // (8 * groups)) * 8
    packed = jnp.pad(packed, ((0, chunk * groups - rows), (0, 0)))
    mine = lax.dynamic_slice_in_dim(packed, lax.axis_index("groups") * chunk, chunk, axis=0)
    everything = lax.all_gather(mine, ("groups", "sp"), axis=0, tiled=False)
    return everything.reshape(groups, lax.axis_size("sp"), chunk, LANES)


def rows_of(everything, start, stop):
    groups, _, chunk, _ = everything.shape
    parts = []
    for g in range(groups):
        low, high = max(start, g * chunk), min(stop, (g + 1) * chunk)
        if low < high:
            parts.append(everything[g, :, low - g * chunk : high - g * chunk])
    return parts[0] if len(parts) == 1 else jnp.concatenate(parts, axis=1)


def attend(query_part, key_part, value_part):
    sp = lax.axis_size("sp")
    batches, rows, width = query_part.shape
    heads = width // HEAD_FEATURES
    both = jnp.stack([query_part, key_part, value_part], axis=1)
    both = both.reshape(batches, 3, rows, heads, HEAD_FEATURES).transpose(0, 3, 1, 2, 4)
    swapped = lax.all_to_all(both, "core", split_axis=0, concat_axis=0, tiled=True)
    to_heads = jnp.swapaxes(swapped, 0, 1).reshape(sp, CORES * 3 * rows, HEAD_FEATURES)
    here = lax.all_to_all(to_heads, "sp", split_axis=0, concat_axis=0, tiled=True)
    here = here.reshape(sp, CORES, 3, rows, HEAD_FEATURES)
    count = sp * CORES * rows
    queries = here[:, :, 0].reshape(count, HEAD_FEATURES)
    own = here[:, :, 1:].transpose(2, 0, 1, 3, 4).reshape(2, count, HEAD_FEATURES)
    gathered = sent_to_all(own, "x")
    keys = gathered[:, 0].reshape(-1, HEAD_FEATURES)
    values = gathered[:, 1].reshape(-1, HEAD_FEATURES)
    scores = contract_last(queries, keys) * (1.0 / math.sqrt(HEAD_FEATURES))
    exponent = jnp.exp(scores - jnp.max(scores, axis=-1, keepdims=True))
    row_total = jnp.sum(exponent, axis=-1, keepdims=True)
    weighted = jnp.dot(
        exponent.astype(jnp.bfloat16), values, preferred_element_type=jnp.float32
    )
    attended = (weighted / row_total).astype(jnp.bfloat16)
    back = attended.reshape(sp, CORES * rows, HEAD_FEATURES)
    return lax.all_to_all(back, "sp", split_axis=0, concat_axis=0, tiled=True)


def body(
    query_rows, key_rows, value_rows, residual, modulation, out_weight, up_weight, down_weight
):
    everything = gathered_weights(out_weight, up_weight, down_weight)
    sp = lax.axis_size("sp")
    tp = ("x", "core")
    tp_size = lax.axis_size(tp)
    batches, rows_block, local_width = residual.shape
    row_count = batches * rows_block
    rows = query_rows.shape[1]
    units = up_weight.shape[1]
    depth = up_weight.shape[0]
    outs = out_weight.shape[0]

    own = attend(query_rows, key_rows, value_rows)
    stripes = sent_to_all(own, tp)
    stripes = stripes.reshape(tp_size // CORES, CORES, sp, CORES * rows, HEAD_FEATURES)
    flat_rows = stripes.transpose(1, 0, 3, 2, 4).reshape(row_count, sp * HEAD_FEATURES)

    out_full = rows_of(everything, 0, outs)
    out_full = jnp.swapaxes(out_full, 0, 1).reshape(outs, sp * LANES)
    projected = contract_last(flat_rows, out_full)
    mixed_rows = (
        residual.reshape(row_count, local_width).astype(jnp.float32) + modulation[0] * projected
    )
    sums = jnp.stack([jnp.sum(mixed_rows, axis=1), jnp.sum(mixed_rows * mixed_rows, axis=1)])
    first_sum, second_sum = jnp.sum(sent_to_all(sums, tp), axis=0)
    row_mean = first_sum / D
    spread = second_sum / D - row_mean * row_mean
    normed = (
        (mixed_rows - row_mean[:, None])
        * lax.rsqrt(spread[:, None] + 1e-06)
        * (1.0 + modulation[2])
        + modulation[1]
    ).astype(jnp.bfloat16)
    columns = jnp.swapaxes(sent_to_all(normed, tp), 0, 1).reshape(row_count, D)

    def unpacked(start):
        part = rows_of(everything, start, start + units // LANES * depth)
        part = part.reshape(sp, units // LANES, depth, LANES).transpose(0, 2, 1, 3)
        return part.reshape(sp * depth, units)

    up_full = unpacked(outs)
    down_full = unpacked(outs + units // LANES * depth)
    hidden = jnp.dot(columns, up_full, preferred_element_type=jnp.float32)
    active = jax.nn.gelu(hidden, approximate=True).astype(jnp.bfloat16)
    partial_out = contract_last(active, down_full).astype(jnp.bfloat16)
    shares = jnp.moveaxis(partial_out.reshape(row_count, tp_size, local_width), 1, 0)
    shares = lax.all_to_all(shares, tp, 0, 0, tiled=True)
    summed = jnp.sum(shares.astype(jnp.float32), axis=0)
    result = (mixed_rows + modulation[3] * summed).astype(jnp.bfloat16)
    return result.reshape(batches, rows_block, local_width)


def solution(mesh):
    groups, tp, sp = (mesh.shape[a] for a in ("groups", "tp", "sp"))
    fine = Mesh(
        mesh.devices.reshape(groups, tp // CORES, CORES, sp), ("groups", "x", "core", "sp")
    )
    tokens, tensor = ("sp", "x", "core"), ("x", "core")
    in_specs = (
        P("groups", tokens, None),
        P("groups", tokens, None),
        P("groups", tokens, None),
        P("groups", "sp", tensor),
        P(None, tensor),
        P(tensor, "sp"),
        P("sp", tensor),
        P("sp", tensor),
    )
    out_specs = P("groups", "sp", tensor)
    return jax.shard_map(body, mesh=fine, in_specs=in_specs, out_specs=out_specs, check_vma=False)
```

time: 619 us -> 465 us (0.75)
  waiting for transfers between devices: 322 us -> 214 us
  blocking collectives: 220 us -> 155 us
  starting transfers between devices: 10.3 us -> 41.9 us
  local copies, waits for them, and re-layouts: 37.8 us -> 25.4 us
    all_gather x4 -> x1, waiting for transfers between devices: 305 us -> 184 us  [gathered_weights(): everything = lax.all_gather(mine, ('groups', 'sp'), axis=0, tiled=False)]
    all_to_all x4, blocking collectives: 220 us -> 155 us  [the longest x1 62.3 us: attend(): lax.all_to_all(to_heads, 'sp', split_axis=0, concat_axis=0, tiled=True)]
    all_to_all x2 -> x4, starting transfers between devices: 10.1 us -> 41.9 us  [sent_to_all(): return lax.all_to_all(copies, axis, split_axis=0, concat_axis=0, tiled=True)]
    unnamed x6 -> x10, local copies, waits for them, and re-layouts: 17.9 us -> 0.99 us
    all_to_all x2 -> x4, waiting for transfers between devices: 14.9 us -> 29.3 us  [sent_to_all(): return lax.all_to_all(copies, axis, split_axis=0, concat_axis=0, tiled=True)]
    transpose x0 -> x6, local copies, waits for them, and re-layouts: none -> 7.7 us  [the longest x2 7.36 us: unpacked(): part = part.reshape(sp, units // LANES, depth, LANES).transpose(0, 2, 1, 3)]
    all_to_all x3 -> x1, local copies, waits for them, and re-layouts: 7.49 us -> 0.15 us  [attend(): lax.all_to_all(both, 'core', split_axis=0, concat_axis=0, tiled=True)]
    concatenate x1 -> x0, local copies, waits for them, and re-layouts: 7.16 us -> none  [in_one_piece(): both = jnp.concatenate(arrays, axis=along)]
  transfers between devices with their start and end apart: 6 -> 5, of which waited for: 5 -> 4; matrix products, arithmetic and copies ran while one was open for 2% -> 5% of each run, Pallas kernels for 0% -> 0%
where the time goes in v1:
time: 465 us; the launch traced here: 464 us
  waiting for transfers between devices  214 us (46%)
  blocking collectives  155 us (33%)
  starting transfers between devices  41.9 us (9%)
  local copies, waits for them, and re-layouts  25.4 us (5%)
  between operations  13.6 us (3%)
  matrix products  10.8 us (2%)
    all_gather x1, waiting for transfers between devices, gathered_weights(): everything = lax.all_gather(mine, ('groups', 'sp'), axis=0, tiled=False)  184 us
    all_to_all x1, blocking collectives, attend(): lax.all_to_all(to_heads, 'sp', split_axis=0, concat_axis=0, tiled=True)  62.3 us
    all_to_all x1, blocking collectives, attend(): lax.all_to_all(both, 'core', split_axis=0, concat_axis=0, tiled=True)  45.1 us
    all_to_all x4, starting transfers between devices, sent_to_all(): return lax.all_to_all(copies, axis, split_axis=0, concat_axis=0, tiled=True)  41.9 us
    all_to_all x1, blocking collectives, attend(): return lax.all_to_all(back, 'sp', split_axis=0, concat_axis=0, tiled=True)  33.1 us
    all_to_all x4, waiting for transfers between devices, sent_to_all(): return lax.all_to_all(copies, axis, split_axis=0, concat_axis=0, tiled=True)  29.3 us
    all_to_all x1, blocking collectives, body(): shares = lax.all_to_all(shares, tp, 0, 0, tiled=True)  14.6 us
    dot_general x3, matrix products, contract_last(): lax.dot_general(left, right, (((1,), (1,)), ((), ())), preferred_element_...  9.95 us
  transfers between devices with their start and end apart: 5, of which 4 were waited for; matrix products, arithmetic and copies ran while one was open for 5% of the time, Pallas kernels for 0%

profile of v1, /device:TPU:33, one launch (start us, length us, event | category | flops | bytes accessed | tf_op | source)
XLA Modules:
  0.0 464.4 jit_solution(24833544857068728)
XLA Ops:
  6.6 1.1 reshape.95
  7.7 1.1 reshape.97
  8.8 2.3 fusion.51
  11.1 0.1 all-gather.3.cloned.1.call-update
  11.1 0.9 copy.113
  12.0 1.0 copy_bitcast_fusion
  13.2 45.1 %all_to_all.40 = bf16[2,32,3,8,128]{4,1,3,2,0:T(8,128)(2,1)S(1)} all-to-all(bf16[2,32,3,8,128]{4,1,3,2,0:T(8,128)(2,1)S(1)} %copy.54), channel_id=1, replica_groups=mesh['groups'=2,'x'=4,'core'=2,'sp'=32] {'core'}, dimensions={0} | all-to-all | bytes 786432 | tf_op jit(solution)/shard_map/all_to_all | solution.py:58
  58.3 0.2 copy.55
  58.4 62.3 %all_to_all.41 = bf16[32,48,128]{2,1,0:T(8,128)(2,1)S(1)} all-to-all(bf16[32,48,128]{2,1,0:T(8,128)(2,1)S(1)} %bitcast.132), channel_id=1, replica_groups=mesh['groups'=2,'x'=4,'core'=2,'sp'=32] {'sp'}, dimensions={0} | all-to-all | bytes 786432 | tf_op jit(solution)/shard_map/all_to_all | solution.py:60
  120.8 1.1 broadcast_in_dim.8
  121.9 4.3 all-to-all-start.2
  126.2 13.5 %all-to-all-done.2 = bf16[4,2,512,128]{3,2,1,0:T(8,128)(2,1)S(1)} async-done(((bf16[4,2,512,128]{3,2,1,0:T(8,128)(2,1)}), bf16[4,2,512,128]{3,2,1,0:T(8,128)(2,1)S(1)}, u32[]{:S(2)}, u32[]{:S(2)}) %all-to-all-start.2) | async-done | bytes 1048608 | tf_op jit(solution)/shard_map/all_to_all | solution.py:22
  139.7 0.1 fusion.60
  139.8 0.8 multiply_reduce_fusion
  140.6 0.8 fusion.9
  141.4 0.0 copy-start.1
  141.4 0.8 fusion.21
  142.3 33.1 %all_to_all.42 = bf16[32,16,128]{2,1,0:T(8,128)(2,1)S(1)} all-to-all(bf16[32,16,128]{2,1,0:T(8,128)(2,1)S(1)} %bitcast.144), channel_id=1, replica_groups=mesh['groups'=2,'x'=4,'core'=2,'sp'=32] {'sp'}, dimensions={0} | all-to-all | bytes 262144 | tf_op jit(solution)/shard_map/all_to_all | solution.py:76
  175.4 1.1 broadcast_in_dim.18
  176.5 8.2 %all-to-all-start.4 = ((bf16[8,32,16,128]{3,2,1,0:T(8,128)(2,1)}), bf16[8,32,16,128]{3,2,1,0:T(8,128)(2,1)S(1)}, u32[]{:S(2)}, u32[]{:S(2)}) async-start(bf16[8,32,16,128]{3,2,1,0:T(8,128)(2,1)} %broadcast_in_dim.18), calls=%async_computation.4 | async-start | bytes 2097152 | tf_op jit(solution)/shard_map/all_to_all | solution.py:22
  184.8 0.1 copy.61
  184.9 0.0 copy-done.1
  184.9 14.9 %all-to-all-done.4 = bf16[8,32,16,128]{3,2,1,0:T(8,128)(2,1)S(1)} async-done(((bf16[8,32,16,128]{3,2,1,0:T(8,128)(2,1)}), bf16[8,32,16,128]{3,2,1,0:T(8,128)(2,1)S(1)}, u32[]{:S(2)}, u32[]{:S(2)}) %all-to-all-start.4) | async-done | bytes 1048608 | tf_op jit(solution)/shard_map/all_to_all | solution.py:22
  199.8 0.3 copy.57
  200.1 184.5 %all-gather.3.cloned.1.call-done = bf16[46080,128]{1,0:T(8,128)(2,1)} async-done(((bf16[720,128]{1,0:T(8,128)(2,1)}), bf16[46080,128]{1,0:T(8,128)(2,1)}) %all-gather.3.cloned.1.call-update) | async-done | bytes 11796496 | tf_op jit(solution)/shard_map/all_gather | solution.py:38
  384.5 2.6 fusion.59
  387.2 0.6 broadcast_in_dim.19
  387.8 24.5 %all-to-all-start.5 = ((f32[8,2,128]{2,1,0:T(2,128)}), f32[8,2,128]{2,1,0:T(2,128)S(1)}, u32[]{:S(2)}, u32[]{:S(2)}) async-start(f32[8,2,128]{2,1,0:T(2,128)} %broadcast_in_dim.19), calls=%async_computation.5 | async-start | bytes 16384 | tf_op jit(solution)/shard_map/all_to_all | solution.py:22
  412.3 1.4 slice_bitcast_fusion.2
  413.7 4.7 %slice.55 = bf16[1,32,560,128]{3,2,1,0:T(8,128)(2,1)} slice(bf16[2,32,720,128]{3,2,1,0:T(8,128)(2,1)} %bitcast.123), slice={[1:2], [0:32], [160:720], [0:128]} | slice | bytes 9175040 | tf_op jit(solution)/shard_map/slice | solution.py:48
  418.4 0.0 all-to-all-done.5
  418.5 0.2 add_convert_fusion.1
  418.6 0.9 broadcast_in_dim.20
  419.6 4.8 %all-to-all-start.6 = ((bf16[8,128,320]{1,2,0:T(8,128)(2,1)}), bf16[8,128,320]{1,2,0:T(8,128)(2,1)S(1)}, u32[]{:S(2)}, u32[]{:S(2)}) async-start(bf16[8,128,320]{1,2,0:T(8,128)(2,1)} %broadcast_in_dim.20), calls=%async_computation.6 | async-start | bytes 1310720 | tf_op jit(solution)/shard_map/all_to_all | solution.py:22
  424.4 2.1 slice_bitcast_fusion
  426.5 0.0 slice-start
  426.5 0.3 pad_maximum_fusion
  426.8 0.0 slice-start.1
  426.8 3.7 copy.63
  430.5 0.0 slice-done
  430.5 3.7 copy.64
  434.2 0.9 all-to-all-done.6
  435.1 6.5 %fusion.6 = bf16[128,2560]{1,0:T(8,128)(2,1)S(1)} fusion(bf16[320,8,7,128]{3,2,1,0:T(8,128)(2,1)} %bitcast.126, bf16[128,2560]{0,1:T(8,128)(2,1)S(1)} %bitcast.135, bf16[320,8,7,128]{3,2,1,0:T(8,128)(2,1)} %bitcast.125), kind=kOutput, calls=%fused_computation.9 | convolution fusion | flops 1175764992 | bytes 10485760 | tf_op jit(solution)/shard_map/dot_general | solution.py:15
  441.7 0.3 copy.65
  442.0 14.6 %all_to_all.43 = bf16[8,128,320]{1,2,0:T(8,128)(2,1)S(1)} all-to-all(bf16[8,128,320]{1,2,0:T(8,128)(2,1)S(1)} %bitcast.128), channel_id=1, replica_groups=mesh['groups'=2,'x'=4,'core'=2,'sp'=32] {'x','core'}, dimensions={0} | all-to-all | bytes 1310720 | tf_op jit(solution)/shard_map/all_to_all | solution.py:127
  456.6 0.1 convert_reduce_fusion
  456.7 0.1 add_convert_fusion
  456.8 0.8 copy.66
  (18 shorter events, 0.3 us)
Async XLA Ops:
  6.5 378.0 %all-gather.3.cloned.1.call-start = ((), (), s32[]{:S(2)}) async-start(), calls=%async_computation.8 | async-start | bytes 11980800 | tf_op jit(solution)/shard_map/all_gather | solution.py:38
  121.9 17.8 %all-to-all-start.2 = ((bf16[4,2,512,128]{3,2,1,0:T(8,128)(2,1)}), bf16[4,2,512,128]{3,2,1,0:T(8,128)(2,1)S(1)}, u32[]{:S(2)}, u32[]{:S(2)}) async-start(bf16[4,2,512,128]{3,2,1,0:T(8,128)(2,1)} %broadcast_in_dim.8), calls=%async_computation.2 | async-start | bytes 2097152 | tf_op jit(solution)/shard_map/all_to_all | solution.py:22
  141.4 43.3 %copy-start = (bf16[2,64,320]{2,1,0:T(8,128)(2,1)S(1)}, bf16[2,64,320]{2,1,0:T(8,128)(2,1)}, u32[]{:S(2)}) copy-start(bf16[2,64,320]{2,1,0:T(8,128)(2,1)} %param.11) | copy-start | bytes 245764
  141.4 43.5 %copy-start.1 = (f32[4,320]{1,0:T(4,128)S(1)}, f32[4,320]{1,0:T(4,128)}, u32[]{:S(2)}) copy-start(f32[4,320]{1,0:T(4,128)} %param.12) | copy-start | bytes 15364
  176.5 23.3 %all-to-all-start.4 = ((bf16[8,32,16,128]{3,2,1,0:T(8,128)(2,1)}), bf16[8,32,16,128]{3,2,1,0:T(8,128)(2,1)S(1)}, u32[]{:S(2)}, u32[]{:S(2)}) async-start(bf16[8,32,16,128]{3,2,1,0:T(8,128)(2,1)} %broadcast_in_dim.18), calls=%async_computation.4 | async-start | bytes 2097152 | tf_op jit(solution)/shard_map/all_to_all | solution.py:22
  387.8 30.6 %all-to-all-start.5 = ((f32[8,2,128]{2,1,0:T(2,128)}), f32[8,2,128]{2,1,0:T(2,128)S(1)}, u32[]{:S(2)}, u32[]{:S(2)}) async-start(f32[8,2,128]{2,1,0:T(2,128)} %broadcast_in_dim.19), calls=%async_computation.5 | async-start | bytes 16384 | tf_op jit(solution)/shard_map/all_to_all | solution.py:22
  419.6 15.6 %all-to-all-start.6 = ((bf16[8,128,320]{1,2,0:T(8,128)(2,1)}), bf16[8,128,320]{1,2,0:T(8,128)(2,1)S(1)}, u32[]{:S(2)}, u32[]{:S(2)}) async-start(bf16[8,128,320]{1,2,0:T(8,128)(2,1)} %broadcast_in_dim.20), calls=%async_computation.6 | async-start | bytes 1310720 | tf_op jit(solution)/shard_map/all_to_all | solution.py:22
  426.5 4.0 slice-start
  426.8 3.7 slice-start.1
Sparse Core Ops, SparseCore 0:
  11.2 373.2 all-gather.2

commit v2 on v1

--- a/solution.py
+++ b/solution.py
@@ -23,30 +23,22 @@
 
 
 def gathered_weights(out_weight, up_weight, down_weight):
-    groups = lax.axis_size("groups")
     depth, units = up_weight.shape
-    pieces = [
-        out_weight,
-        jnp.swapaxes(up_weight.reshape(depth, units // LANES, LANES), 0, 1).reshape(-1, LANES),
-        jnp.swapaxes(down_weight.reshape(depth, units // LANES, LANES), 0, 1).reshape(-1, LANES),
-    ]
-    packed = jnp.concatenate(pieces, axis=0)
-    rows = packed.shape[0]
-    chunk = -(-rows // (8 * groups)) * 8
-    packed = jnp.pad(packed, ((0, chunk * groups - rows), (0, 0)))
-    mine = lax.dynamic_slice_in_dim(packed, lax.axis_index("groups") * chunk, chunk, axis=0)
-    everything = lax.all_gather(mine, ("groups", "sp"), axis=0, tiled=False)
-    return everything.reshape(groups, lax.axis_size("sp"), chunk, LANES)
+    packed = jnp.concatenate(
+        [
+            out_weight.reshape(-1, depth, LANES),
+            jnp.swapaxes(up_weight.reshape(depth, units // LANES, LANES), 0, 1),
+            jnp.swapaxes(down_weight.reshape(depth, units // LANES, LANES), 0, 1),
+        ],
+        axis=0,
+    )
+    return lax.all_gather(packed, "sp", axis=1, tiled=True)
 
 
-def rows_of(everything, start, stop):
-    groups, _, chunk, _ = everything.shape
-    parts = []
-    for g in range(groups):
-        low, high = max(start, g * chunk), min(stop, (g + 1) * chunk)
-        if low < high:
-            parts.append(everything[g, :, low - g * chunk : high - g * chunk])
-    return parts[0] if len(parts) == 1 else jnp.concatenate(parts, axis=1)
+def in_two(array):
+    high = lax.reduce_precision(array, 8, 7)
+    low = lax.reduce_precision(array - high, 8, 7)
+    return high, low
 
 
 def attend(query_part, key_part, value_part):
@@ -86,43 +78,56 @@
     batches, rows_block, local_width = residual.shape
     row_count = batches * rows_block
     rows = query_rows.shape[1]
-    units = up_weight.shape[1]
-    depth = up_weight.shape[0]
-    outs = out_weight.shape[0]
+    depth, units = up_weight.shape
+    out_pieces, unit_pieces = local_width // depth, units // LANES
 
     own = attend(query_rows, key_rows, value_rows)
-    stripes = sent_to_all(own, tp)
-    stripes = stripes.reshape(tp_size // CORES, CORES, sp, CORES * rows, HEAD_FEATURES)
-    flat_rows = stripes.transpose(1, 0, 3, 2, 4).reshape(row_count, sp * HEAD_FEATURES)
+    own = own.reshape(-1, HEAD_FEATURES)
+    shift_scale = jnp.stack(in_two(modulation[1:3])).astype(jnp.bfloat16).reshape(-1, LANES)
+    extra = -shift_scale.shape[0] % 16
+    message = jnp.concatenate([own, jnp.pad(shift_scale, ((0, extra), (0, 0)))], axis=0)
+    stripes = sent_to_all(message, tp)
+    halves = stripes[:, own.shape[0] : own.shape[0] + shift_scale.shape[0]]
+    halves = halves.reshape(tp_size, 2, 2, local_width).astype(jnp.float32)
+    shift, scale = (halves[:, 0, k] + halves[:, 1, k] for k in range(2))
+    stripes = stripes[:, : own.shape[0]].reshape(
+        tp_size // CORES, CORES, sp, CORES * rows, HEAD_FEATURES
+    )
+    flat_rows = stripes.transpose(1, 0, 3, 2, 4).reshape(row_count, sp, HEAD_FEATURES)
 
-    out_full = rows_of(everything, 0, outs)
-    out_full = jnp.swapaxes(out_full, 0, 1).reshape(outs, sp * LANES)
-    projected = contract_last(flat_rows, out_full)
+    out_full = everything[:out_pieces].reshape(out_pieces, sp, depth, LANES)
+    projected = jnp.einsum(
+        "rsf,psif->rpi", flat_rows, out_full, preferred_element_type=jnp.float32
+    ).reshape(row_count, local_width)
     mixed_rows = (
         residual.reshape(row_count, local_width).astype(jnp.float32) + modulation[0] * projected
     )
-    sums = jnp.stack([jnp.sum(mixed_rows, axis=1), jnp.sum(mixed_rows * mixed_rows, axis=1)])
-    first_sum, second_sum = jnp.sum(sent_to_all(sums, tp), axis=0)
-    row_mean = first_sum / D
-    spread = second_sum / D - row_mean * row_mean
+    high, low = in_two(jnp.mean(mixed_rows, axis=1, keepdims=True))
+    deviation = mixed_rows - (high + low)
+    message = jnp.concatenate(
+        [deviation, high, low, jnp.zeros((row_count, 14), jnp.float32)], axis=1
+    ).astype(jnp.bfloat16)
+    spreads = sent_to_all(message, tp).astype(jnp.float32)
+    spreads = (
+        spreads[:, :, :local_width]
+        + spreads[:, :, local_width : local_width + 1]
+        + spreads[:, :, local_width + 1 : local_width + 2]
+    )
+    row_mean = jnp.mean(spreads, axis=(0, 2), keepdims=True)
+    centred = spreads - row_mean
+    spread = jnp.mean(centred * centred, axis=(0, 2), keepdims=True)
     normed = (
-        (mixed_rows - row_mean[:, None])
-        * lax.rsqrt(spread[:, None] + 1e-06)
-        * (1.0 + modulation[2])
-        + modulation[1]
+        centred * lax.rsqrt(spread + 1e-06) * (1.0 + scale[:, None]) + shift[:, None]
     ).astype(jnp.bfloat16)
-    columns = jnp.swapaxes(sent_to_all(normed, tp), 0, 1).reshape(row_count, D)
+    columns = jnp.swapaxes(normed, 0, 1).reshape(row_count, D)
 
-    def unpacked(start):
-        part = rows_of(everything, start, start + units // LANES * depth)
-        part = part.reshape(sp, units // LANES, depth, LANES).transpose(0, 2, 1, 3)
-        return part.reshape(sp * depth, units)
-
-    up_full = unpacked(outs)
-    down_full = unpacked(outs + units // LANES * depth)
-    hidden = jnp.dot(columns, up_full, preferred_element_type=jnp.float32)
+    up_full = everything[out_pieces : out_pieces + unit_pieces]
+    down_full = everything[out_pieces + unit_pieces :]
+    hidden = jnp.einsum("rk,jkn->rjn", columns, up_full, preferred_element_type=jnp.float32)
     active = jax.nn.gelu(hidden, approximate=True).astype(jnp.bfloat16)
-    partial_out = contract_last(active, down_full).astype(jnp.bfloat16)
+    partial_out = jnp.einsum(
+        "rjn,jon->ro", active, down_full, preferred_element_type=jnp.float32
+    ).astype(jnp.bfloat16)
     shares = jnp.moveaxis(partial_out.reshape(row_count, tp_size, local_width), 1, 0)
     shares = lax.all_to_all(shares, tp, 0, 0, tiled=True)
     summed = jnp.sum(shares.astype(jnp.float32), axis=0)

time: 465 us -> 293 us (0.63)
  waiting for transfers between devices: 214 us -> 99.8 us
  blocking collectives: 155 us -> 121 us
  local copies, waits for them, and re-layouts: 25.4 us -> 11.7 us
  starting transfers between devices: 41.9 us -> 30.8 us
    all_gather x1, waiting for transfers between devices: 184 us -> 31.3 us  [gathered_weights(): return lax.all_gather(packed, 'sp', axis=1, tiled=True)]
    all_to_all x1 -> x0, blocking collectives: 33.1 us -> none  [attend(): return lax.all_to_all(back, 'sp', split_axis=0, concat_axis=0, tiled=True)]
    all_to_all x0 -> x1, waiting for transfers between devices: none -> 31 us  [attend(): return lax.all_to_all(back, 'sp', split_axis=0, concat_axis=0, tiled=True)]
    all_to_all x4 -> x3, starting transfers between devices: 41.9 us -> 24.5 us  [sent_to_all(): return lax.all_to_all(copies, axis, split_axis=0, concat_axis=0, tiled=True)]
    dot_general x3 -> x1, matrix products: 9.95 us -> 0.79 us  [contract_last(): lax.dot_general(left, right, (((1,), (1,)), ((), ())), preferred_element_...]
    all_to_all x4 -> x3, waiting for transfers between devices: 29.3 us -> 37.5 us  [sent_to_all(): return lax.all_to_all(copies, axis, split_axis=0, concat_axis=0, tiled=True)]
    dot_general x0 -> x2, matrix products: none -> 6.93 us  [the longest x1 6.08 us: body(): jnp.einsum('rjn,jon->ro', active, down_full, preferred_element_type=jnp.f...]
    all_to_all x0 -> x1, starting transfers between devices: none -> 6.22 us  [attend(): return lax.all_to_all(back, 'sp', split_axis=0, concat_axis=0, tiled=True)]
  transfers between devices with their start and end apart: 5 -> 5, of which waited for: 4 -> 5; matrix products, arithmetic and copies ran while one was open for 5% -> 3% of each run, Pallas kernels for 0% -> 0%
where the time goes in v2:
time: 293 us; the launch traced here: 292 us
  blocking collectives  121 us (41%)
  waiting for transfers between devices  99.8 us (34%)
  starting transfers between devices  30.8 us (11%)
  between operations  13.7 us (5%)
  local copies, waits for them, and re-layouts  11.7 us (4%)
  matrix products  9.2 us (3%)
  other arithmetic  5.44 us (2%)
    all_to_all x1, blocking collectives, attend(): lax.all_to_all(to_heads, 'sp', split_axis=0, concat_axis=0, tiled=True)  61.9 us
    all_to_all x1, blocking collectives, attend(): lax.all_to_all(both, 'core', split_axis=0, concat_axis=0, tiled=True)  45.1 us
    all_to_all x3, waiting for transfers between devices, sent_to_all(): return lax.all_to_all(copies, axis, split_axis=0, concat_axis=0, tiled=True)  37.5 us
    all_gather x1, waiting for transfers between devices, gathered_weights(): return lax.all_gather(packed, 'sp', axis=1, tiled=True)  31.3 us
    all_to_all x1, waiting for transfers between devices, attend(): return lax.all_to_all(back, 'sp', split_axis=0, concat_axis=0, tiled=True)  31 us
    all_to_all x3, starting transfers between devices, sent_to_all(): return lax.all_to_all(copies, axis, split_axis=0, concat_axis=0, tiled=True)  24.5 us
    all_to_all x1, blocking collectives, body(): shares = lax.all_to_all(shares, tp, 0, 0, tiled=True)  14.3 us
    all_to_all x1, starting transfers between devices, attend(): return lax.all_to_all(back, 'sp', split_axis=0, concat_axis=0, tiled=True)  6.22 us
  transfers between devices with their start and end apart: 5, of which 5 were waited for; matrix products, arithmetic and copies ran while one was open for 3% of the time, Pallas kernels for 0%

profile of v2, /device:TPU:33, one launch (start us, length us, event | category | flops | bytes accessed | tf_op | source)
XLA Modules:
  0.0 292.0 jit_solution(16005638108837977002)
XLA Ops:
  6.6 0.1 all-gather.2.cloned.1.call-start
  6.6 0.8 copy-done
  7.5 1.0 bitcast_bitcast_fusion
  8.4 1.7 pad_maximum_fusion
  10.4 45.1 %all_to_all.35 = bf16[2,32,3,8,128]{4,1,3,2,0:T(8,128)(2,1)S(1)} all-to-all(bf16[2,32,3,8,128]{4,1,3,2,0:T(8,128)(2,1)S(1)} %copy.38), channel_id=1, replica_groups=mesh['groups'=2,'x'=4,'core'=2,'sp'=32] {'core'}, dimensions={0} | all-to-all | bytes 786432 | tf_op jit(solution)/shard_map/all_to_all | solution.py:50
  55.5 0.2 copy.39
  55.6 61.9 %all_to_all.36 = bf16[32,48,128]{2,1,0:T(8,128)(2,1)S(1)} all-to-all(bf16[32,48,128]{2,1,0:T(8,128)(2,1)S(1)} %bitcast.105), channel_id=1, replica_groups=mesh['groups'=2,'x'=4,'core'=2,'sp'=32] {'sp'}, dimensions={0} | all-to-all | bytes 786432 | tf_op jit(solution)/shard_map/all_to_all | solution.py:52
  117.6 1.1 broadcast_in_dim.8
  118.8 4.0 %all-to-all-start.2 = ((bf16[4,2,512,128]{3,2,1,0:T(8,128)(2,1)}), bf16[4,2,512,128]{3,2,1,0:T(8,128)(2,1)S(1)}, u32[]{:S(2)}, u32[]{:S(2)}) async-start(bf16[4,2,512,128]{3,2,1,0:T(8,128)(2,1)} %broadcast_in_dim.8), calls=%async_computation.2 | async-start | bytes 2097152 | tf_op jit(solution)/shard_map/all_to_all | solution.py:22
  122.8 12.4 %all-to-all-done.2 = bf16[4,2,512,128]{3,2,1,0:T(8,128)(2,1)S(1)} async-done(((bf16[4,2,512,128]{3,2,1,0:T(8,128)(2,1)}), bf16[4,2,512,128]{3,2,1,0:T(8,128)(2,1)S(1)}, u32[]{:S(2)}, u32[]{:S(2)}) %all-to-all-start.2) | async-done | bytes 1048608 | tf_op jit(solution)/shard_map/all_to_all | solution.py:22
  135.2 0.1 fusion.60
  135.2 0.8 multiply_reduce_fusion
  136.0 0.8 fusion.10
  136.9 1.5 fusion.20
  138.4 6.2 %all-to-all-start.3 = ((bf16[32,16,128]{2,1,0:T(8,128)(2,1)}), bf16[32,16,128]{2,1,0:T(8,128)(2,1)S(1)}, u32[]{:S(2)}, u32[]{:S(2)}) async-start(bf16[32,16,128]{2,1,0:T(8,128)(2,1)} %bitcast.10), calls=%async_computation.3 | async-start | bytes 262144 | tf_op jit(solution)/shard_map/all_to_all | solution.py:68
  144.6 0.1 convert_element_type.48
  144.7 31.0 %all-to-all-done.3 = bf16[32,16,128]{2,1,0:T(8,128)(2,1)S(1)} async-done(((bf16[32,16,128]{2,1,0:T(8,128)(2,1)}), bf16[32,16,128]{2,1,0:T(8,128)(2,1)S(1)}, u32[]{:S(2)}, u32[]{:S(2)}) %all-to-all-start.3) | async-done | bytes 131104 | tf_op jit(solution)/shard_map/all_to_all | solution.py:68
  175.7 1.2 broadcast_in_dim.9
  176.8 6.5 %all-to-all-start.4 = ((bf16[8,528,128]{2,1,0:T(8,128)(2,1)}), bf16[8,528,128]{2,1,0:T(8,128)(2,1)S(1)}, u32[]{:S(2)}, u32[]{:S(2)}) async-start(bf16[8,528,128]{2,1,0:T(8,128)(2,1)} %broadcast_in_dim.9), calls=%async_computation.4 | async-start | bytes 2162688 | tf_op jit(solution)/shard_map/all_to_all | solution.py:22
  183.4 0.1 copy.45
  183.5 0.1 pad.8.clone
  183.6 15.2 %all-to-all-done.4 = bf16[8,528,128]{2,1,0:T(8,128)(2,1)S(1)} async-done(((bf16[8,528,128]{2,1,0:T(8,128)(2,1)}), bf16[8,528,128]{2,1,0:T(8,128)(2,1)S(1)}, u32[]{:S(2)}, u32[]{:S(2)}) %all-to-all-start.4) | async-done | bytes 1081376 | tf_op jit(solution)/shard_map/all_to_all | solution.py:22
  198.7 0.1 slice.80
  198.8 1.4 copy.41
  200.2 31.3 %all-gather.2.cloned.1.call-done = bf16[18,2560,128]{2,1,0:T(8,128)(2,1)} async-done(((bf16[18,80,128]{2,1,0:T(8,128)(2,1)}), bf16[18,2560,128]{2,1,0:T(8,128)(2,1)}) %all-gather.2.cloned.1.call-update) | async-done | bytes 11796496 | tf_op jit(solution)/shard_map/all_gather | solution.py:35
  231.5 1.7 slice-done
  233.3 0.3 copy.44
  233.6 0.9 copy-done.2
  234.5 0.8 fusion.61
  235.4 0.1 maximum_maximum_fusion
  235.5 1.0 broadcast_in_dim.22
  236.5 14.0 %all-to-all-start.5 = ((bf16[8,128,336]{1,2,0:T(8,128)(2,1)}), bf16[8,128,336]{1,2,0:T(8,128)(2,1)S(1)}, u32[]{:S(2)}, u32[]{:S(2)}) async-start(bf16[8,128,336]{1,2,0:T(8,128)(2,1)} %broadcast_in_dim.22), calls=%async_computation.5 | async-start | bytes 1376256 | tf_op jit(solution)/shard_map/all_to_all | solution.py:22
  250.5 0.8 slice_convert_fusion
  251.3 0.1 reshape.143
  251.4 0.1 copy.54
  251.6 0.1 copy.55
  251.7 9.9 %all-to-all-done.5 = bf16[8,128,336]{1,2,0:T(8,128)(2,1)S(1)} async-done(((bf16[8,128,336]{1,2,0:T(8,128)(2,1)}), bf16[8,128,336]{1,2,0:T(8,128)(2,1)S(1)}, u32[]{:S(2)}, u32[]{:S(2)}) %all-to-all-start.5) | async-done | bytes 688160 | tf_op jit(solution)/shard_map/all_to_all | solution.py:22
  261.6 0.1 copy_convert_fusion
  261.8 0.4 fusion.25
  262.1 0.4 multiply_reduce_fusion.1
  262.5 0.8 fusion.26
  263.4 0.1 copy.49
  263.4 6.1 %fusion.7 = bf16[128,2560]{1,0:T(8,128)(2,1)S(1)} fusion(bf16[18,2560,128]{2,1,0:T(8,128)(2,1)} %all-gather.2.cloned.1.call-done, bf16[128,2560,1]{0,1,2:T(8,128)(2,1)S(1)} %bitcast.109), kind=kOutput, calls=%fused_computation.7 | convolution fusion | flops 1175764992 | bytes 10485760 | tf_op jit(solution)/shard_map/rjn,jon->ro/dot_general | solution.py:128
  269.5 0.3 copy.51
  269.9 14.3 %all_to_all.37 = bf16[8,128,320]{1,2,0:T(8,128)(2,1)S(1)} all-to-all(bf16[8,128,320]{1,2,0:T(8,128)(2,1)S(1)} %bitcast.101), channel_id=1, replica_groups=mesh['groups'=2,'x'=4,'core'=2,'sp'=32] {'x','core'}, dimensions={0} | all-to-all | bytes 1310720 | tf_op jit(solution)/shard_map/all_to_all | solution.py:132
  284.2 0.1 convert_reduce_fusion
  284.3 0.1 add_convert_fusion.1
  284.4 0.8 copy.52
  (36 shorter events, 0.5 us)
Async XLA Ops:
  6.5 0.9 copy-start
  6.6 3.6 %copy-start.3 = (bf16[2,8,4096]{2,1,0:T(8,128)(2,1)S(1)}, bf16[2,8,4096]{2,1,0:T(8,128)(2,1)}, u32[]{:S(2)}) copy-start(bf16[2,8,4096]{2,1,0:T(8,128)(2,1)} %param.8) | copy-start | bytes 393220
  6.6 3.6 %copy-start.5 = (bf16[2,8,4096]{2,1,0:T(8,128)(2,1)S(1)}, bf16[2,8,4096]{2,1,0:T(8,128)(2,1)}, u32[]{:S(2)}) copy-start(bf16[2,8,4096]{2,1,0:T(8,128)(2,1)} %param.9) | copy-start | bytes 393220
  6.6 3.6 %copy-start.4 = (bf16[2,8,4096]{2,1,0:T(8,128)(2,1)S(1)}, bf16[2,8,4096]{2,1,0:T(8,128)(2,1)}, u32[]{:S(2)}) copy-start(bf16[2,8,4096]{2,1,0:T(8,128)(2,1)} %param.10) | copy-start | bytes 393220
  6.6 225.0 %all-gather.2.cloned.1.call-start = ((), (), s32[]{:S(2)}) async-start(), calls=%async_computation.7 | async-start | bytes 12165120 | tf_op jit(solution)/shard_map/all_gather | solution.py:35
  118.8 16.4 %all-to-all-start.2 = ((bf16[4,2,512,128]{3,2,1,0:T(8,128)(2,1)}), bf16[4,2,512,128]{3,2,1,0:T(8,128)(2,1)S(1)}, u32[]{:S(2)}, u32[]{:S(2)}) async-start(bf16[4,2,512,128]{3,2,1,0:T(8,128)(2,1)} %broadcast_in_dim.8), calls=%async_computation.2 | async-start | bytes 2097152 | tf_op jit(solution)/shard_map/all_to_all | solution.py:22
  136.9 7.7 %copy-start.7 = (f32[4,320]{1,0:T(4,128)S(1)}, f32[4,320]{1,0:T(4,128)}, u32[]{:S(2)}) copy-start(f32[4,320]{1,0:T(4,128)} %param.12) | copy-start | bytes 15364
  138.4 37.3 %all-to-all-start.3 = ((bf16[32,16,128]{2,1,0:T(8,128)(2,1)}), bf16[32,16,128]{2,1,0:T(8,128)(2,1)S(1)}, u32[]{:S(2)}, u32[]{:S(2)}) async-start(bf16[32,16,128]{2,1,0:T(8,128)(2,1)} %bitcast.10), calls=%async_computation.3 | async-start | bytes 262144 | tf_op jit(solution)/shard_map/all_to_all | solution.py:68
  176.8 6.5 %copy-start.6 = (bf16[2,64,320]{2,1,0:T(8,128)(2,1)S(1)}, bf16[2,64,320]{2,1,0:T(8,128)(2,1)}, u32[]{:S(2)}) copy-start(bf16[2,64,320]{2,1,0:T(8,128)(2,1)} %param.11) | copy-start | bytes 245764
  176.8 21.9 %all-to-all-start.4 = ((bf16[8,528,128]{2,1,0:T(8,128)(2,1)}), bf16[8,528,128]{2,1,0:T(8,128)(2,1)S(1)}, u32[]{:S(2)}, u32[]{:S(2)}) async-start(bf16[8,528,128]{2,1,0:T(8,128)(2,1)} %broadcast_in_dim.9), calls=%async_computation.4 | async-start | bytes 2162688 | tf_op jit(solution)/shard_map/all_to_all | solution.py:22
  198.7 1.4 copy-start.1
  231.5 1.7 slice-start
  233.3 1.2 copy-start.2
  236.5 25.1 %all-to-all-start.5 = ((bf16[8,128,336]{1,2,0:T(8,128)(2,1)}), bf16[8,128,336]{1,2,0:T(8,128)(2,1)S(1)}, u32[]{:S(2)}, u32[]{:S(2)}) async-start(bf16[8,128,336]{1,2,0:T(8,128)(2,1)} %broadcast_in_dim.22), calls=%async_computation.5 | async-start | bytes 1376256 | tf_op jit(solution)/shard_map/all_to_all | solution.py:22
Sparse Core Ops, SparseCore 0:
  10.3 221.1 all-gather.1

commit v3 on v2

v3 whole, which is shorter than its diff:
```python
import functools
import math

import jax
import jax.numpy as jnp
from jax import lax
from jax.experimental import pallas as pl
from jax.experimental.pallas import tpu as pltpu
from jax.sharding import Mesh, PartitionSpec as P

HEAD_FEATURES = 128
LANES = 128
CORES = 2
MEBI = 1 << 20
LIMIT = 48


def contract_last(left, right):
    return lax.dot_general(
        left, right, (((1,), (1,)), ((), ())), preferred_element_type=jnp.float32
    )


def sent_to_all(array, axis):
    copies = jnp.broadcast_to(array, (lax.axis_size(axis), *array.shape))
    return lax.all_to_all(copies, axis, split_axis=0, concat_axis=0, tiled=True)


def gathered_weights(out_weight, up_weight, down_weight):
    depth, units = up_weight.shape
    packed = jnp.concatenate(
        [
            out_weight,
            jnp.swapaxes(up_weight.reshape(depth, units // LANES, LANES), 0, 1).reshape(-1, LANES),
            jnp.swapaxes(down_weight.reshape(depth, units // LANES, LANES), 0, 1).reshape(-1, LANES),
        ],
        axis=0,
    )
    return lax.all_gather(packed, "sp", axis=0, tiled=False)


def in_two(array):
    high = lax.reduce_precision(array, 8, 7)
    low = lax.reduce_precision(array - high, 8, 7)
    return high, low


def attend(query_part, key_part, value_part):
    sp = lax.axis_size("sp")
    batches, rows, width = query_part.shape
    heads = width // HEAD_FEATURES
    both = jnp.stack([query_part, key_part, value_part], axis=1)
    both = both.reshape(batches, 3, rows, heads, HEAD_FEATURES).transpose(0, 3, 1, 2, 4)
    swapped = lax.all_to_all(both, "core", split_axis=0, concat_axis=0, tiled=True)
    to_heads = jnp.swapaxes(swapped, 0, 1).reshape(sp, CORES * 3 * rows, HEAD_FEATURES)
    here = lax.all_to_all(to_heads, "sp", split_axis=0, concat_axis=0, tiled=True)
    here = here.reshape(sp, CORES, 3, rows, HEAD_FEATURES)
    count = sp * CORES * rows
    queries = here[:, :, 0].reshape(count, HEAD_FEATURES)
    own = here[:, :, 1:].transpose(2, 0, 1, 3, 4).reshape(2, count, HEAD_FEATURES)
    gathered = sent_to_all(own, "x")
    keys = gathered[:, 0].reshape(-1, HEAD_FEATURES)
    values = gathered[:, 1].reshape(-1, HEAD_FEATURES)
    scores = contract_last(queries, keys) * (1.0 / math.sqrt(HEAD_FEATURES))
    exponent = jnp.exp(scores - jnp.max(scores, axis=-1, keepdims=True))
    row_total = jnp.sum(exponent, axis=-1, keepdims=True)
    weighted = jnp.dot(
        exponent.astype(jnp.bfloat16), values, preferred_element_type=jnp.float32
    )
    attended = (weighted / row_total).astype(jnp.bfloat16)
    back = attended.reshape(sp, CORES * rows, HEAD_FEATURES)
    return lax.all_to_all(back, "sp", split_axis=0, concat_axis=0, tiled=True)


def project_kernel(
    parts, stripes_ref, weights_ref, residual_ref, modulation_ref, mixed_ref, message_ref, held, sems
):
    heads, outs, _ = held.shape
    tp_size = stripes_ref.shape[0]
    each = heads // parts
    copies = [
        pltpu.make_async_copy(
            weights_ref.at[pl.ds(k * each, each), pl.ds(0, outs), :],
            held.at[pl.ds(k * each, each)],
            sems.at[k],
        )
        for k in range(parts)
    ]
    for copy in copies:
        copy.start()
    batches, rows_block, _ = residual_ref.shape
    span = batches * rows_block // tp_size
    residual = jnp.concatenate(
        [
            residual_ref[t % batches, t // batches * span : (t // batches + 1) * span, :]
            for t in range(tp_size)
        ],
        axis=0,
    ).astype(jnp.float32)
    total = jnp.zeros(residual.shape, jnp.float32)
    for k in range(parts):
        copies[k].wait()
        for h in range(k * each, (k + 1) * each, 2):
            left, right = (
                jnp.concatenate(pair, axis=1)
                for pair in (
                    [
                        stripes_ref[:, i * span : (i + 1) * span, :].reshape(-1, LANES)
                        for i in (h, h + 1)
                    ],
                    [held[h], held[h + 1]],
                )
            )
            total = total + contract_last(left, right)
    mixed = residual + modulation_ref[0:1, :] * total
    mixed_ref[...] = mixed
    mean = jnp.mean(mixed, axis=1, keepdims=True)
    high = mean.astype(jnp.bfloat16)
    low = (mean - high.astype(jnp.float32)).astype(jnp.bfloat16)
    deviation = mixed - (high.astype(jnp.float32) + low.astype(jnp.float32))
    width = mixed.shape[1]
    message_ref[:, 0:width] = deviation.astype(jnp.bfloat16)
    rest = message_ref.shape[1] - width
    lane = lax.broadcasted_iota(jnp.int32, (mixed.shape[0], rest), 1)
    message_ref[:, width:] = jnp.where(
        lane == 0, high.astype(jnp.float32), jnp.where(lane == 1, low.astype(jnp.float32), 0.0)
    ).astype(jnp.bfloat16)


def project(stripes, everything, residual, modulation):
    outs = modulation.shape[1]
    rows = residual.shape[0] * residual.shape[1]
    sp = everything.shape[0]
    parts = 4
    vmem = pl.BlockSpec(memory_space=pltpu.VMEM)
    return pl.pallas_call(
        functools.partial(project_kernel, parts),
        out_shape=(
            jax.ShapeDtypeStruct((rows, outs), jnp.float32),
            jax.ShapeDtypeStruct((rows, -(-(outs + 2) // LANES) * LANES), jnp.bfloat16),
        ),
        in_specs=[vmem, pl.BlockSpec(memory_space=pltpu.HBM), vmem, vmem],
        out_specs=(vmem, vmem),
        scratch_shapes=[
            pltpu.VMEM((sp, outs, LANES), jnp.bfloat16),
            pltpu.SemaphoreType.DMA((parts,)),
        ],
        compiler_params=pltpu.CompilerParams(vmem_limit_bytes=LIMIT * MEBI),
        name="project",
    )(stripes, everything, residual, modulation)


def feed_kernel(outs, messages_ref, scales_ref, weights_ref, shares_ref, ups, downs, sems):
    sp, depth, units = ups.shape
    pieces = units // LANES
    tp_size, rows, _ = messages_ref.shape
    copies = []
    for matrix, held in enumerate((ups, downs)):
        for j in range(pieces):
            k = matrix * pieces + j
            copies.append(
                pltpu.make_async_copy(
                    weights_ref.at[:, pl.ds(outs + k * depth, depth), :],
                    held.at[:, :, pl.ds(j * LANES, LANES)],
                    sems.at[k],
                )
            )
    for copy in copies:
        copy.start()
    spreads = []
    for t in range(tp_size):
        mean = messages_ref[t, :, outs : outs + 2].astype(jnp.float32)
        spreads.append(
            messages_ref[t, :, 0:outs].astype(jnp.float32) + (mean[:, 0:1] + mean[:, 1:2])
        )
    features = tp_size * outs
    row_mean = sum(jnp.sum(part, axis=1, keepdims=True) for part in spreads) / features
    centred = [part - row_mean for part in spreads]
    spread = sum(jnp.sum(part * part, axis=1, keepdims=True) for part in centred) / features
    factor = lax.rsqrt(spread + 1e-06)
    normed = jnp.concatenate(
        [
            centred[t] * factor * (1.0 + scales_ref[1, t : t + 1, :]) + scales_ref[0, t : t + 1, :]
            for t in range(tp_size)
        ],
        axis=1,
    ).astype(jnp.bfloat16)
    active = []
    for j in range(0, pieces, 2):
        stop = min(j + 2, pieces)
        for k in range(j, stop):
            copies[k].wait()
        block = ups[:, :, j * LANES : stop * LANES].reshape(sp * depth, -1)
        hidden = jnp.dot(normed, block, preferred_element_type=jnp.float32)
        active.append(jax.nn.gelu(hidden, approximate=True).astype(jnp.bfloat16))
    active = jnp.concatenate(active, axis=1)
    for copy in copies[pieces:]:
        copy.wait()
    each = sp // tp_size
    for t in range(tp_size):
        block = downs[t * each : (t + 1) * each].reshape(each * depth, units)
        shares_ref[t] = contract_last(block, active).astype(jnp.bfloat16)


def feed(messages, scales, everything, depth, units):
    tp_size, rows, _ = messages.shape
    outs = scales.shape[2]
    sp = everything.shape[0]
    vmem = pl.BlockSpec(memory_space=pltpu.VMEM)
    return pl.pallas_call(
        functools.partial(feed_kernel, outs),
        out_shape=jax.ShapeDtypeStruct((tp_size, outs, rows), jnp.bfloat16),
        in_specs=[vmem, vmem, pl.BlockSpec(memory_space=pltpu.HBM)],
        out_specs=vmem,
        scratch_shapes=[
            pltpu.VMEM((sp, depth, units), jnp.bfloat16),
            pltpu.VMEM((sp, depth, units), jnp.bfloat16),
            pltpu.SemaphoreType.DMA((2 * units // LANES,)),
        ],
        compiler_params=pltpu.CompilerParams(vmem_limit_bytes=LIMIT * MEBI),
        name="feed",
    )(messages, scales, everything)


def finish_kernel(shares_ref, mixed_ref, modulation_ref, out_ref):
    tp_size, outs, rows = shares_ref.shape
    batches = out_ref.shape[0]
    span = rows // tp_size
    total = jnp.zeros((outs, rows), jnp.float32)
    for t in range(tp_size):
        total = total + shares_ref[t].astype(jnp.float32)
    rest = -outs % LANES
    turned = jnp.concatenate([total, jnp.zeros((rest, rows), jnp.float32)], axis=0).T[:, :outs]
    result = (mixed_ref[...] + modulation_ref[3:4, :] * turned).astype(jnp.bfloat16)
    for t in range(tp_size):
        place = t // batches * span
        out_ref[t % batches, place : place + span, :] = result[t * span : (t + 1) * span]


def body(
    query_rows, key_rows, value_rows, residual, modulation, out_weight, up_weight, down_weight
):
    everything = gathered_weights(out_weight, up_weight, down_weight)
    tp = ("x", "core")
    tp_size = lax.axis_size(tp)
    local_width = residual.shape[2]
    depth, units = up_weight.shape

    own = attend(query_rows, key_rows, value_rows)
    own = own.reshape(-1, HEAD_FEATURES)
    shift_scale = jnp.stack(in_two(modulation[1:3])).astype(jnp.bfloat16).reshape(-1, LANES)
    extra = -shift_scale.shape[0] % 16
    message = jnp.concatenate([own, jnp.pad(shift_scale, ((0, extra), (0, 0)))], axis=0)
    stripes = sent_to_all(message, tp)
    halves = stripes[:, own.shape[0] : own.shape[0] + shift_scale.shape[0]]
    halves = halves.reshape(tp_size, 2, 2, local_width).astype(jnp.float32)
    scales = jnp.swapaxes(halves[:, 0] + halves[:, 1], 0, 1)

    mixed, message = project(stripes, everything, residual, modulation)
    messages = lax.all_gather(message, tp, axis=0, tiled=False)
    shares = feed(messages, scales, everything, depth, units)
    shares = lax.all_to_all(shares, tp, 0, 0, tiled=True)
    return pl.pallas_call(
        finish_kernel,
        out_shape=jax.ShapeDtypeStruct(residual.shape, residual.dtype),
        compiler_params=pltpu.CompilerParams(vmem_limit_bytes=8 * MEBI),
        name="finish",
    )(shares, mixed, modulation)


def solution(mesh):
    groups, tp, sp = (mesh.shape[a] for a in ("groups", "tp", "sp"))
    fine = Mesh(
        mesh.devices.reshape(groups, tp // CORES, CORES, sp), ("groups", "x", "core", "sp")
    )
    tokens, tensor = ("sp", "x", "core"), ("x", "core")
    in_specs = (
        P("groups", tokens, None),
        P("groups", tokens, None),
        P("groups", tokens, None),
        P("groups", "sp", tensor),
        P(None, tensor),
        P(tensor, "sp"),
        P("sp", tensor),
        P("sp", tensor),
    )
    out_specs = P("groups", "sp", tensor)
    return jax.shard_map(body, mesh=fine, in_specs=in_specs, out_specs=out_specs, check_vma=False)
```

time: 293 us -> 288 us (0.983)
  blocking collectives: 121 us -> 167 us
  waiting for transfers between devices: 99.8 us -> 77 us
  starting transfers between devices: 30.8 us -> 10.3 us
  Pallas kernels: 0 us -> 8.78 us
  matrix products: 9.2 us -> 2.27 us
  local copies, waits for them, and re-layouts: 11.7 us -> 5.99 us
    all_to_all x3 -> x1, waiting for transfers between devices: 37.5 us -> 12.6 us  [sent_to_all(): return lax.all_to_all(copies, axis, split_axis=0, concat_axis=0, tiled=True)]
    all_gather x0 -> x1, blocking collectives: none -> 24.2 us  [body(): messages = lax.all_gather(message, tp, axis=0, tiled=False)]
    all_to_all x0 -> x1, blocking collectives: none -> 21.4 us  [sent_to_all(): return lax.all_to_all(copies, axis, split_axis=0, concat_axis=0, tiled=True)]
    all_to_all x3 -> x1, starting transfers between devices: 24.5 us -> 4.42 us  [sent_to_all(): return lax.all_to_all(copies, axis, split_axis=0, concat_axis=0, tiled=True)]
    pallas_call x0 -> x3, Pallas kernels: none -> 8.78 us  [the longest x1 5.11 us: feed(): pl.pallas_call(functools.partial(feed_kernel, outs), out_shape=jax.ShapeD...]
    dot_general x2 -> x0, matrix products: 6.93 us -> none  [the longest x1 6.08 us: body(): jnp.einsum('rjn,jon->ro', active, down_full, preferred_element_type=jnp.f...]
  transfers between devices with their start and end apart: 5 -> 3, of which waited for: 5 -> 3; matrix products, arithmetic and copies ran while one was open for 3% -> 2% of each run, Pallas kernels for 0% -> 0%
where the time goes in v3:
time: 288 us; the launch traced here: 287 us
  blocking collectives  167 us (58%)
  waiting for transfers between devices  77 us (27%)
  between operations  13.6 us (5%)
  starting transfers between devices  10.3 us (4%)
  Pallas kernels  8.78 us (3%)
  local copies, waits for them, and re-layouts  5.99 us (2%)
    all_to_all x1, blocking collectives, attend(): lax.all_to_all(to_heads, 'sp', split_axis=0, concat_axis=0, tiled=True)  61.5 us
    all_to_all x1, blocking collectives, attend(): lax.all_to_all(both, 'core', split_axis=0, concat_axis=0, tiled=True)  45.1 us
    all_gather x1, waiting for transfers between devices, gathered_weights(): return lax.all_gather(packed, 'sp', axis=0, tiled=False)  33.6 us
    all_to_all x1, waiting for transfers between devices, attend(): return lax.all_to_all(back, 'sp', split_axis=0, concat_axis=0, tiled=True)  30.8 us
    all_gather x1, blocking collectives, body(): messages = lax.all_gather(message, tp, axis=0, tiled=False)  24.2 us
    all_to_all x1, blocking collectives, sent_to_all(): return lax.all_to_all(copies, axis, split_axis=0, concat_axis=0, tiled=True)  21.4 us
    all_to_all x1, blocking collectives, body(): shares = lax.all_to_all(shares, tp, 0, 0, tiled=True)  14.7 us
    all_to_all x1, waiting for transfers between devices, sent_to_all(): return lax.all_to_all(copies, axis, split_axis=0, concat_axis=0, tiled=True)  12.6 us
  transfers between devices with their start and end apart: 3, of which 3 were waited for; matrix products, arithmetic and copies ran while one was open for 2% of the time, Pallas kernels for 0%

profile of v3, /device:TPU:33, one launch (start us, length us, event | category | flops | bytes accessed | tf_op | source)
XLA Modules:
  0.0 287.4 jit_solution(9344834205136139770)
XLA Ops:
  6.5 0.0 all-gather.4.cloned.1.call-start
  6.6 1.1 reshape.48
  7.7 1.1 reshape.50
  8.8 1.7 pad_maximum_fusion
  10.5 0.1 all-gather.4.cloned.1.call-update
  10.6 0.9 copy.40
  11.5 1.0 copy_bitcast_fusion
  12.6 45.1 %all_to_all.30 = bf16[2,32,3,8,128]{4,1,3,2,0:T(8,128)(2,1)S(1)} all-to-all(bf16[2,32,3,8,128]{4,1,3,2,0:T(8,128)(2,1)S(1)} %copy.20), channel_id=1, replica_groups=mesh['groups'=2,'x'=4,'core'=2,'sp'=32] {'core'}, dimensions={0} | all-to-all | bytes 786432 | tf_op jit(solution)/shard_map/all_to_all | solution.py:54
  57.7 0.2 copy.21
  57.9 61.5 %all_to_all.31 = bf16[32,48,128]{2,1,0:T(8,128)(2,1)S(1)} all-to-all(bf16[32,48,128]{2,1,0:T(8,128)(2,1)S(1)} %bitcast.56), channel_id=1, replica_groups=mesh['groups'=2,'x'=4,'core'=2,'sp'=32] {'sp'}, dimensions={0} | all-to-all | bytes 786432 | tf_op jit(solution)/shard_map/all_to_all | solution.py:56
  119.5 1.1 broadcast_in_dim.8
  120.6 4.4 %all-to-all-start.2 = ((bf16[4,2,512,128]{3,2,1,0:T(8,128)(2,1)}), bf16[4,2,512,128]{3,2,1,0:T(8,128)(2,1)S(1)}, u32[]{:S(2)}, u32[]{:S(2)}) async-start(bf16[4,2,512,128]{3,2,1,0:T(8,128)(2,1)} %broadcast_in_dim.8), calls=%async_computation.2 | async-start | bytes 2097152 | tf_op jit(solution)/shard_map/all_to_all | solution.py:26
  125.1 12.6 %all-to-all-done.2 = bf16[4,2,512,128]{3,2,1,0:T(8,128)(2,1)S(1)} async-done(((bf16[4,2,512,128]{3,2,1,0:T(8,128)(2,1)}), bf16[4,2,512,128]{3,2,1,0:T(8,128)(2,1)S(1)}, u32[]{:S(2)}, u32[]{:S(2)}) %all-to-all-start.2) | async-done | bytes 1048608 | tf_op jit(solution)/shard_map/all_to_all | solution.py:26
  137.7 0.1 fusion.20
  137.7 0.8 multiply_reduce_fusion
  138.5 0.0 copy-start.1
  138.5 0.8 fusion
  139.3 0.0 copy-start
  139.4 1.5 fusion.9
  140.8 5.9 %all-to-all-start.3 = ((bf16[32,16,128]{2,1,0:T(8,128)(2,1)}), bf16[32,16,128]{2,1,0:T(8,128)(2,1)S(1)}, u32[]{:S(2)}, u32[]{:S(2)}) async-start(bf16[32,16,128]{2,1,0:T(8,128)(2,1)} %bitcast.9), calls=%async_computation.3 | async-start | bytes 262144 | tf_op jit(solution)/shard_map/all_to_all | solution.py:72
  146.7 0.0 copy-done.1
  146.7 0.1 convert_element_type.21
  146.8 30.8 %all-to-all-done.3 = bf16[32,16,128]{2,1,0:T(8,128)(2,1)S(1)} async-done(((bf16[32,16,128]{2,1,0:T(8,128)(2,1)}), bf16[32,16,128]{2,1,0:T(8,128)(2,1)S(1)}, u32[]{:S(2)}, u32[]{:S(2)}) %all-to-all-start.3) | async-done | bytes 131104 | tf_op jit(solution)/shard_map/all_to_all | solution.py:72
  177.6 0.1 broadcast_in_dim.9
  177.8 21.4 %all_to_all.32.stripes_ref = bf16[8,528,128]{2,1,0:T(8,128)(2,1)S(1)} all-to-all(bf16[8,528,128]{2,1,0:T(8,128)(2,1)S(1)} %broadcast_in_dim.9), channel_id=1, replica_groups=mesh['groups'=2,'x'=4,'core'=2,'sp'=32] {'x','core'}, dimensions={0} | all-to-all | bytes 2162688 | tf_op jit(solution)/shard_map/all_to_all | solution.py:26
  199.2 0.1 reshape.52
  199.3 33.6 %all-gather.4.cloned.1.call-done = bf16[46080,128]{1,0:T(8,128)(2,1)} async-done(((bf16[1440,128]{1,0:T(8,128)(2,1)}), bf16[46080,128]{1,0:T(8,128)(2,1)}) %all-gather.4.cloned.1.call-update) | async-done | bytes 11796496 | tf_op jit(solution)/shard_map/all_gather | solution.py:39
  232.9 0.0 copy-done
  232.9 2.9 project.1
  235.8 24.2 %all-gather.1 = bf16[1024,384]{1,0:T(8,128)(2,1)S(1)} all-gather(bf16[128,384]{1,0:T(8,128)(2,1)S(1)} %get-tuple-element.7), channel_id=3, replica_groups=mesh['groups'=2,'x'=4,'core'=2,'sp'=32] {'x','core'}, dimensions={0}, use_global_device_ids=true | all-gather | bytes 884736 | tf_op jit(solution)/shard_map/all_gather | solution.py:260
  259.9 5.1 %feed.1 = bf16[8,320,128]{2,1,0:T(8,128)(2,1)S(1)} custom-call(bf16[8,128,384]{2,1,0:T(8,128)(2,1)S(1)} %bitcast.50, f32[2,8,320]{2,1,0:T(8,128)S(1)} %fusion.14.scales_ref, bf16[32,1440,128]{2,1,0:T(8,128)(2,1)} %bitcast.52), custom_call_target="tpu_custom_call" | custom-call | tf_op jit(solution)/shard_map/feed/pallas_call | solution.py:210
  265.1 14.7 %all_to_all.33.shares_ref = bf16[8,320,128]{2,1,0:T(8,128)(2,1)S(1)} all-to-all(bf16[8,320,128]{2,1,0:T(8,128)(2,1)S(1)} %feed.1), channel_id=1, replica_groups=mesh['groups'=2,'x'=4,'core'=2,'sp'=32] {'x','core'}, dimensions={0} | all-to-all | bytes 1310720 | tf_op jit(solution)/shard_map/all_to_all | solution.py:262
  279.7 0.8 finish.1
  (13 shorter events, 0.3 us)
Async XLA Ops:
  6.5 226.3 %all-gather.4.cloned.1.call-start = ((), (), s32[]{:S(2)}) async-start(), calls=%async_computation.6 | async-start | bytes 12165120 | tf_op jit(solution)/shard_map/all_gather | solution.py:39
  120.6 17.0 %all-to-all-start.2 = ((bf16[4,2,512,128]{3,2,1,0:T(8,128)(2,1)}), bf16[4,2,512,128]{3,2,1,0:T(8,128)(2,1)S(1)}, u32[]{:S(2)}, u32[]{:S(2)}) async-start(bf16[4,2,512,128]{3,2,1,0:T(8,128)(2,1)} %broadcast_in_dim.8), calls=%async_computation.2 | async-start | bytes 2097152 | tf_op jit(solution)/shard_map/all_to_all | solution.py:26
  138.5 8.2 %copy-start.1 = (f32[4,320]{1,0:T(4,128)S(1)}, f32[4,320]{1,0:T(4,128)}, u32[]{:S(2)}) copy-start(f32[4,320]{1,0:T(4,128)} %modulation_ref.3) | copy-start | bytes 15364
  139.3 93.6 %copy-start = (bf16[2,64,320]{2,1,0:T(8,128)(2,1)S(1)}, bf16[2,64,320]{2,1,0:T(8,128)(2,1)}, u32[]{:S(2)}) copy-start(bf16[2,64,320]{2,1,0:T(8,128)(2,1)} %residual_ref.1) | copy-start | bytes 245764
  140.8 36.7 %all-to-all-start.3 = ((bf16[32,16,128]{2,1,0:T(8,128)(2,1)}), bf16[32,16,128]{2,1,0:T(8,128)(2,1)S(1)}, u32[]{:S(2)}, u32[]{:S(2)}) async-start(bf16[32,16,128]{2,1,0:T(8,128)(2,1)} %bitcast.9), calls=%async_computation.3 | async-start | bytes 262144 | tf_op jit(solution)/shard_map/all_to_all | solution.py:72
Sparse Core Ops, SparseCore 0:
  10.7 222.1 all-gather.3

commit v4 on v3

--- a/solution.py
+++ b/solution.py
@@ -13,6 +13,7 @@
 CORES = 2
 MEBI = 1 << 20
 LIMIT = 48
+MEAN_PARTS = 3
 
 
 def contract_last(left, right):
@@ -115,29 +116,31 @@
     mixed = residual + modulation_ref[0:1, :] * total
     mixed_ref[...] = mixed
     mean = jnp.mean(mixed, axis=1, keepdims=True)
-    high = mean.astype(jnp.bfloat16)
-    low = (mean - high.astype(jnp.float32)).astype(jnp.bfloat16)
-    deviation = mixed - (high.astype(jnp.float32) + low.astype(jnp.float32))
+    left, told, places = mean, jnp.zeros_like(mean), []
+    for _ in range(MEAN_PARTS):
+        places.append(left.astype(jnp.bfloat16).astype(jnp.float32))
+        told = told + places[-1]
+        left = mean - told
     width = mixed.shape[1]
-    message_ref[:, 0:width] = deviation.astype(jnp.bfloat16)
-    rest = message_ref.shape[1] - width
-    lane = lax.broadcasted_iota(jnp.int32, (mixed.shape[0], rest), 1)
-    message_ref[:, width:] = jnp.where(
-        lane == 0, high.astype(jnp.float32), jnp.where(lane == 1, low.astype(jnp.float32), 0.0)
-    ).astype(jnp.bfloat16)
+    lane = lax.broadcasted_iota(jnp.int32, (mixed.shape[0], -width % LANES), 1)
+    means = jnp.zeros(lane.shape, jnp.float32)
+    for k, place in enumerate(places):
+        means = jnp.where(lane == k, place, means)
+    turned = jnp.concatenate([mixed - told, means], axis=1).T
+    message_ref[...] = turned[: message_ref.shape[0]].astype(jnp.bfloat16)
 
 
 def project(stripes, everything, residual, modulation):
     outs = modulation.shape[1]
     rows = residual.shape[0] * residual.shape[1]
     sp = everything.shape[0]
-    parts = 4
+    parts = 8
     vmem = pl.BlockSpec(memory_space=pltpu.VMEM)
     return pl.pallas_call(
         functools.partial(project_kernel, parts),
         out_shape=(
             jax.ShapeDtypeStruct((rows, outs), jnp.float32),
-            jax.ShapeDtypeStruct((rows, -(-(outs + 2) // LANES) * LANES), jnp.bfloat16),
+            jax.ShapeDtypeStruct((outs + 16, rows), jnp.bfloat16),
         ),
         in_specs=[vmem, pl.BlockSpec(memory_space=pltpu.HBM), vmem, vmem],
         out_specs=(vmem, vmem),
@@ -150,72 +153,75 @@
     )(stripes, everything, residual, modulation)
 
 
-def feed_kernel(outs, messages_ref, scales_ref, weights_ref, shares_ref, ups, downs, sems):
+def feed_kernel(messages_ref, scales_ref, weights_ref, shares_ref, ups, downs, sems):
     sp, depth, units = ups.shape
     pieces = units // LANES
-    tp_size, rows, _ = messages_ref.shape
-    copies = []
-    for matrix, held in enumerate((ups, downs)):
-        for j in range(pieces):
-            k = matrix * pieces + j
-            copies.append(
-                pltpu.make_async_copy(
-                    weights_ref.at[:, pl.ds(outs + k * depth, depth), :],
-                    held.at[:, :, pl.ds(j * LANES, LANES)],
-                    sems.at[k],
-                )
-            )
-    for copy in copies:
+    tp_size = messages_ref.shape[0]
+    features = scales_ref.shape[1]
+    outs = features // tp_size
+    half = sp // 2
+
+    def copy_of(held, k, j, start, count, sem):
+        return pltpu.make_async_copy(
+            weights_ref.at[pl.ds(start, count), pl.ds(outs + k * depth, depth), :],
+            held.at[pl.ds(start, count), :, pl.ds(j * LANES, LANES)],
+            sems.at[sem],
+        )
+
+    up_copies = [copy_of(ups, j, j, 0, sp, j) for j in range(pieces)]
+    down_copies = [
+        [
+            copy_of(downs, pieces + j, j, side * half, half, (1 + side) * pieces + j)
+            for j in range(pieces)
+        ]
+        for side in range(2)
+    ]
+    for copy in [*up_copies, *down_copies[0], *down_copies[1]]:
         copy.start()
     spreads = []
     for t in range(tp_size):
-        mean = messages_ref[t, :, outs : outs + 2].astype(jnp.float32)
-        spreads.append(
-            messages_ref[t, :, 0:outs].astype(jnp.float32) + (mean[:, 0:1] + mean[:, 1:2])
+        mean = jnp.sum(
+            messages_ref[t, outs : outs + 16, :].astype(jnp.float32), axis=0, keepdims=True
         )
-    features = tp_size * outs
-    row_mean = sum(jnp.sum(part, axis=1, keepdims=True) for part in spreads) / features
+        spreads.append(messages_ref[t, 0:outs, :].astype(jnp.float32) + mean)
+    row_mean = sum(jnp.sum(part, axis=0, keepdims=True) for part in spreads) / features
     centred = [part - row_mean for part in spreads]
-    spread = sum(jnp.sum(part * part, axis=1, keepdims=True) for part in centred) / features
+    spread = sum(jnp.sum(part * part, axis=0, keepdims=True) for part in centred) / features
     factor = lax.rsqrt(spread + 1e-06)
-    normed = jnp.concatenate(
-        [
-            centred[t] * factor * (1.0 + scales_ref[1, t : t + 1, :]) + scales_ref[0, t : t + 1, :]
-            for t in range(tp_size)
-        ],
-        axis=1,
-    ).astype(jnp.bfloat16)
+    turned = jnp.concatenate([part * factor for part in centred], axis=0).T
+    normed = (turned * (1.0 + scales_ref[1:2, :]) + scales_ref[0:1, :]).astype(jnp.bfloat16)
     active = []
     for j in range(0, pieces, 2):
         stop = min(j + 2, pieces)
         for k in range(j, stop):
-            copies[k].wait()
+            up_copies[k].wait()
         block = ups[:, :, j * LANES : stop * LANES].reshape(sp * depth, -1)
         hidden = jnp.dot(normed, block, preferred_element_type=jnp.float32)
         active.append(jax.nn.gelu(hidden, approximate=True).astype(jnp.bfloat16))
     active = jnp.concatenate(active, axis=1)
-    for copy in copies[pieces:]:
-        copy.wait()
     each = sp // tp_size
-    for t in range(tp_size):
-        block = downs[t * each : (t + 1) * each].reshape(each * depth, units)
-        shares_ref[t] = contract_last(block, active).astype(jnp.bfloat16)
+    for side in range(2):
+        for copy in down_copies[side]:
+            copy.wait()
+        for t in range(side * tp_size // 2, (side + 1) * tp_size // 2):
+            block = downs[t * each : (t + 1) * each].reshape(each * depth, units)
+            shares_ref[t] = contract_last(block, active).astype(jnp.bfloat16)
 
 
 def feed(messages, scales, everything, depth, units):
-    tp_size, rows, _ = messages.shape
-    outs = scales.shape[2]
+    tp_size, _, rows = messages.shape
+    outs = scales.shape[1] // tp_size
     sp = everything.shape[0]
     vmem = pl.BlockSpec(memory_space=pltpu.VMEM)
     return pl.pallas_call(
-        functools.partial(feed_kernel, outs),
+        feed_kernel,
         out_shape=jax.ShapeDtypeStruct((tp_size, outs, rows), jnp.bfloat16),
         in_specs=[vmem, vmem, pl.BlockSpec(memory_space=pltpu.HBM)],
         out_specs=vmem,
         scratch_shapes=[
             pltpu.VMEM((sp, depth, units), jnp.bfloat16),
             pltpu.VMEM((sp, depth, units), jnp.bfloat16),
-            pltpu.SemaphoreType.DMA((2 * units // LANES,)),
+            pltpu.SemaphoreType.DMA((3 * units // LANES,)),
         ],
         compiler_params=pltpu.CompilerParams(vmem_limit_bytes=LIMIT * MEBI),
         name="feed",
@@ -254,7 +260,7 @@
     stripes = sent_to_all(message, tp)
     halves = stripes[:, own.shape[0] : own.shape[0] + shift_scale.shape[0]]
     halves = halves.reshape(tp_size, 2, 2, local_width).astype(jnp.float32)
-    scales = jnp.swapaxes(halves[:, 0] + halves[:, 1], 0, 1)
+    scales = jnp.swapaxes(halves[:, 0] + halves[:, 1], 0, 1).reshape(2, -1)
 
     mixed, message = project(stripes, everything, residual, modulation)
     messages = lax.all_gather(message, tp, axis=0, tiled=False)

time: 288 us -> 287 us (level)
  no operation moved by 1% of the time
where the time goes in v4:
time: 287 us
  blocking collectives  166 us (58%)
  waiting for transfers between devices  77.3 us (27%)
  between operations  13.6 us (5%)
  starting transfers between devices  10.3 us (4%)
  Pallas kernels  8.84 us (3%)
  local copies, waits for them, and re-layouts  6.07 us (2%)
    all_to_all x1, blocking collectives, attend(): lax.all_to_all(to_heads, 'sp', split_axis=0, concat_axis=0, tiled=True)  61.5 us
    all_to_all x1, blocking collectives, attend(): lax.all_to_all(both, 'core', split_axis=0, concat_axis=0, tiled=True)  45.1 us
    all_gather x1, waiting for transfers between devices, gathered_weights(): return lax.all_gather(packed, 'sp', axis=0, tiled=False)  33.8 us
    all_to_all x1, waiting for transfers between devices, attend(): return lax.all_to_all(back, 'sp', split_axis=0, concat_axis=0, tiled=True)  30.9 us
    all_gather x1, blocking collectives, body(): messages = lax.all_gather(message, tp, axis=0, tiled=False)  23.1 us
    all_to_all x1, blocking collectives, sent_to_all(): return lax.all_to_all(copies, axis, split_axis=0, concat_axis=0, tiled=True)  21.2 us
    all_to_all x1, blocking collectives, body(): shares = lax.all_to_all(shares, tp, 0, 0, tiled=True)  15 us
    all_to_all x1, waiting for transfers between devices, sent_to_all(): return lax.all_to_all(copies, axis, split_axis=0, concat_axis=0, tiled=True)  12.6 us
  transfers between devices with their start and end apart: 3, of which 3 were waited for; matrix products, arithmetic and copies ran while one was open for 2% of the time, Pallas kernels for 0%

profile of v4, /device:TPU:33, one launch (start us, length us, event | category | flops | bytes accessed | tf_op | source)
XLA Modules:
  0.0 286.9 jit_solution(17660202041035929864)
XLA Ops:
  6.5 0.0 all-gather.4.cloned.1.call-start
  6.6 1.1 reshape.51
  7.7 1.1 reshape.53
  8.8 1.7 pad_maximum_fusion
  10.5 0.1 all-gather.4.cloned.1.call-update
  10.5 0.9 copy.33
  11.5 1.0 copy_bitcast_fusion
  12.6 45.1 %all_to_all.30 = bf16[2,32,3,8,128]{4,1,3,2,0:T(8,128)(2,1)S(1)} all-to-all(bf16[2,32,3,8,128]{4,1,3,2,0:T(8,128)(2,1)S(1)} %copy.20), channel_id=1, replica_groups=mesh['groups'=2,'x'=4,'core'=2,'sp'=32] {'core'}, dimensions={0} | all-to-all | bytes 786432 | tf_op jit(solution)/shard_map/all_to_all | solution.py:55
  57.7 0.2 copy.21
  57.9 61.5 %all_to_all.31 = bf16[32,48,128]{2,1,0:T(8,128)(2,1)S(1)} all-to-all(bf16[32,48,128]{2,1,0:T(8,128)(2,1)S(1)} %bitcast.56), channel_id=1, replica_groups=mesh['groups'=2,'x'=4,'core'=2,'sp'=32] {'sp'}, dimensions={0} | all-to-all | bytes 786432 | tf_op jit(solution)/shard_map/all_to_all | solution.py:57
  119.5 1.1 broadcast_in_dim.8
  120.6 4.4 %all-to-all-start.2 = ((bf16[4,2,512,128]{3,2,1,0:T(8,128)(2,1)}), bf16[4,2,512,128]{3,2,1,0:T(8,128)(2,1)S(1)}, u32[]{:S(2)}, u32[]{:S(2)}) async-start(bf16[4,2,512,128]{3,2,1,0:T(8,128)(2,1)} %broadcast_in_dim.8), calls=%async_computation.2 | async-start | bytes 2097152 | tf_op jit(solution)/shard_map/all_to_all | solution.py:27
  125.1 12.6 %all-to-all-done.2 = bf16[4,2,512,128]{3,2,1,0:T(8,128)(2,1)S(1)} async-done(((bf16[4,2,512,128]{3,2,1,0:T(8,128)(2,1)}), bf16[4,2,512,128]{3,2,1,0:T(8,128)(2,1)S(1)}, u32[]{:S(2)}, u32[]{:S(2)}) %all-to-all-start.2) | async-done | bytes 1048608 | tf_op jit(solution)/shard_map/all_to_all | solution.py:27
  137.6 0.1 fusion.20
  137.7 0.8 multiply_reduce_fusion
  138.5 0.0 copy-start.1
  138.5 0.8 fusion
  139.3 0.0 copy-start
  139.3 1.5 fusion.9
  140.8 5.9 %all-to-all-start.3 = ((bf16[32,16,128]{2,1,0:T(8,128)(2,1)}), bf16[32,16,128]{2,1,0:T(8,128)(2,1)S(1)}, u32[]{:S(2)}, u32[]{:S(2)}) async-start(bf16[32,16,128]{2,1,0:T(8,128)(2,1)} %bitcast.9), calls=%async_computation.3 | async-start | bytes 262144 | tf_op jit(solution)/shard_map/all_to_all | solution.py:73
  146.7 0.0 copy-done.1
  146.8 0.1 convert_element_type.21
  146.8 30.9 %all-to-all-done.3 = bf16[32,16,128]{2,1,0:T(8,128)(2,1)S(1)} async-done(((bf16[32,16,128]{2,1,0:T(8,128)(2,1)}), bf16[32,16,128]{2,1,0:T(8,128)(2,1)S(1)}, u32[]{:S(2)}, u32[]{:S(2)}) %all-to-all-start.3) | async-done | bytes 131104 | tf_op jit(solution)/shard_map/all_to_all | solution.py:73
  177.8 0.1 broadcast_in_dim.9
  177.9 21.2 %all_to_all.32.stripes_ref = bf16[8,528,128]{2,1,0:T(8,128)(2,1)S(1)} all-to-all(bf16[8,528,128]{2,1,0:T(8,128)(2,1)S(1)} %broadcast_in_dim.9), channel_id=1, replica_groups=mesh['groups'=2,'x'=4,'core'=2,'sp'=32] {'x','core'}, dimensions={0} | all-to-all | bytes 2162688 | tf_op jit(solution)/shard_map/all_to_all | solution.py:27
  199.2 0.1 reshape.56
  199.3 0.1 reshape.55.scales_ref
  199.4 33.8 %all-gather.4.cloned.1.call-done = bf16[46080,128]{1,0:T(8,128)(2,1)} async-done(((bf16[1440,128]{1,0:T(8,128)(2,1)}), bf16[46080,128]{1,0:T(8,128)(2,1)}) %all-gather.4.cloned.1.call-update) | async-done | bytes 11796496 | tf_op jit(solution)/shard_map/all_gather | solution.py:40
  233.2 0.0 copy-done
  233.2 3.0 %project.1 = (f32[128,320]{1,0:T(8,128)S(1)}, bf16[336,128]{1,0:T(8,128)(2,1)S(1)}) custom-call(bf16[8,528,128]{2,1,0:T(8,128)(2,1)S(1)} %all_to_all.32.stripes_ref, bf16[32,1440,128]{2,1,0:T(8,128)(2,1)} %bitcast.51, bf16[2,64,320]{2,1,0:T(8,128)(2,1)S(1)} %copy-done, f32[4,320]{1,0:T(4,128)S(1)} %copy-done.1), custom_call_target="tpu_custom_call" | custom-call | tf_op jit(solution)/shard_map/project/pallas_call | solution.py:139
  236.2 23.1 %all-gather.1 = bf16[2688,128]{1,0:T(8,128)(2,1)S(1)} all-gather(bf16[336,128]{1,0:T(8,128)(2,1)S(1)} %get-tuple-element.7), channel_id=3, replica_groups=mesh['groups'=2,'x'=4,'core'=2,'sp'=32] {'x','core'}, dimensions={0}, use_global_device_ids=true | all-gather | bytes 774144 | tf_op jit(solution)/shard_map/all_gather | solution.py:266
  259.2 5.0 %feed.1 = bf16[8,320,128]{2,1,0:T(8,128)(2,1)S(1)} custom-call(bf16[8,336,128]{2,1,0:T(8,128)(2,1)S(1)} %bitcast.50, f32[2,2560]{1,0:T(2,128)S(1)} %reshape.55.scales_ref, bf16[32,1440,128]{2,1,0:T(8,128)(2,1)} %bitcast.52), custom_call_target="tpu_custom_call" | custom-call | tf_op jit(solution)/shard_map/feed/pallas_call | solution.py:216
  264.3 15.0 %all_to_all.33.shares_ref = bf16[8,320,128]{2,1,0:T(8,128)(2,1)S(1)} all-to-all(bf16[8,320,128]{2,1,0:T(8,128)(2,1)S(1)} %feed.1), channel_id=1, replica_groups=mesh['groups'=2,'x'=4,'core'=2,'sp'=32] {'x','core'}, dimensions={0} | all-to-all | bytes 1310720 | tf_op jit(solution)/shard_map/all_to_all | solution.py:268
  279.3 0.8 finish.1
  (13 shorter events, 0.3 us)
Async XLA Ops:
  6.5 226.6 %all-gather.4.cloned.1.call-start = ((), (), s32[]{:S(2)}) async-start(), calls=%async_computation.6 | async-start | bytes 12165120 | tf_op jit(solution)/shard_map/all_gather | solution.py:40
  120.6 17.0 %all-to-all-start.2 = ((bf16[4,2,512,128]{3,2,1,0:T(8,128)(2,1)}), bf16[4,2,512,128]{3,2,1,0:T(8,128)(2,1)S(1)}, u32[]{:S(2)}, u32[]{:S(2)}) async-start(bf16[4,2,512,128]{3,2,1,0:T(8,128)(2,1)} %broadcast_in_dim.8), calls=%async_computation.2 | async-start | bytes 2097152 | tf_op jit(solution)/shard_map/all_to_all | solution.py:27
  138.5 8.2 %copy-start.1 = (f32[4,320]{1,0:T(4,128)S(1)}, f32[4,320]{1,0:T(4,128)}, u32[]{:S(2)}) copy-start(f32[4,320]{1,0:T(4,128)} %modulation_ref.3) | copy-start | bytes 15364
  139.3 93.8 %copy-start = (bf16[2,64,320]{2,1,0:T(8,128)(2,1)S(1)}, bf16[2,64,320]{2,1,0:T(8,128)(2,1)}, u32[]{:S(2)}) copy-start(bf16[2,64,320]{2,1,0:T(8,128)(2,1)} %residual_ref.1) | copy-start | bytes 245764
  140.8 36.9 %all-to-all-start.3 = ((bf16[32,16,128]{2,1,0:T(8,128)(2,1)}), bf16[32,16,128]{2,1,0:T(8,128)(2,1)S(1)}, u32[]{:S(2)}, u32[]{:S(2)}) async-start(bf16[32,16,128]{2,1,0:T(8,128)(2,1)} %bitcast.9), calls=%async_computation.3 | async-start | bytes 262144 | tf_op jit(solution)/shard_map/all_to_all | solution.py:73
Sparse Core Ops, SparseCore 0:
  10.7 222.4 all-gather.3

commit v5 on v4

v5 whole, which is shorter than its diff:
```python
import functools
import math

import jax
import jax.numpy as jnp
from jax import lax
from jax.experimental import pallas as pl
from jax.experimental.pallas import tpu as pltpu
from jax.sharding import Mesh, PartitionSpec as P

HEAD_FEATURES = 128
LANES = 128
CORES = 2
PAIR = 2
MEBI = 1 << 20
LIMIT = 48
MEAN_PARTS = 3


def contract_last(left, right):
    return lax.dot_general(
        left, right, (((1,), (1,)), ((), ())), preferred_element_type=jnp.float32
    )


def sent_to_all(array, axis):
    copies = jnp.broadcast_to(array, (lax.axis_size(axis), *array.shape))
    return lax.all_to_all(copies, axis, split_axis=0, concat_axis=0, tiled=True)


def gathered_weights(out_weight, up_weight, down_weight, side):
    depth, units = up_weight.shape
    outs = out_weight.shape[0]

    def half(array, dim):
        size = array.shape[dim] // PAIR
        parts = [lax.slice_in_dim(array, k * size, (k + 1) * size, axis=dim) for k in range(PAIR)]
        return jnp.where(side == 0, parts[0], parts[1])

    up_half, down_half = half(up_weight, 1), half(down_weight, 1)
    whole = units // PAIR // LANES * LANES
    pieces = [half(out_weight, 0)]
    for matrix in (up_half, down_half):
        for start in range(0, whole, LANES):
            pieces.append(matrix[:, start : start + LANES])
    pieces.append(jnp.concatenate([up_half[:, whole:], down_half[:, whole:]], axis=1))
    packed = jnp.concatenate(pieces, axis=0)
    everything = lax.all_gather(packed, ("sp", "core"), axis=0, tiled=False)
    return everything.reshape(lax.axis_size("sp"), CORES, *packed.shape)


def attend(query_part, key_part, value_part):
    sp = lax.axis_size("sp")
    batches, rows, width = query_part.shape
    heads = width // HEAD_FEATURES
    both = jnp.stack([query_part, key_part, value_part], axis=1)
    both = both.reshape(batches, 3, rows, heads, HEAD_FEATURES).transpose(0, 3, 1, 2, 4)
    swapped = lax.all_to_all(both, "core", split_axis=0, concat_axis=0, tiled=True)
    to_heads = jnp.swapaxes(swapped, 0, 1).reshape(sp, CORES * 3 * rows, HEAD_FEATURES)
    here = lax.all_to_all(to_heads, "sp", split_axis=0, concat_axis=0, tiled=True)
    here = here.reshape(sp, CORES, 3, rows, HEAD_FEATURES)
    count = sp * CORES * rows
    queries = here[:, :, 0].reshape(count, HEAD_FEATURES)
    own = here[:, :, 1:].transpose(2, 0, 1, 3, 4).reshape(2, count, HEAD_FEATURES)
    gathered = sent_to_all(own, "x")
    keys = gathered[:, 0].reshape(-1, HEAD_FEATURES)
    values = gathered[:, 1].reshape(-1, HEAD_FEATURES)
    scores = contract_last(queries, keys) * (1.0 / math.sqrt(HEAD_FEATURES))
    exponent = jnp.exp(scores - jnp.max(scores, axis=-1, keepdims=True))
    row_total = jnp.sum(exponent, axis=-1, keepdims=True)
    weighted = jnp.dot(
        exponent.astype(jnp.bfloat16), values, preferred_element_type=jnp.float32
    )
    attended = (weighted / row_total).astype(jnp.bfloat16)
    back = attended.reshape(sp, CORES * rows, HEAD_FEATURES)
    return lax.all_to_all(back, "sp", split_axis=0, concat_axis=0, tiled=True)


def project_kernel(
    parts, place_ref, stripes_ref, weights_ref, residual_ref, gate_ref, placed_ref, message_ref, held, sems
):
    heads, _, half, _ = held.shape
    width = CORES * half
    each = heads // parts
    copies = [
        pltpu.make_async_copy(
            weights_ref.at[pl.ds(k * each, each), :, pl.ds(0, half), :],
            held.at[pl.ds(k * each, each)],
            sems.at[k],
        )
        for k in range(parts)
    ]
    for copy in copies:
        copy.start()
    sources = stripes_ref.shape[0]
    rows = residual_ref.shape[0]
    span = rows // sources
    residual = residual_ref[...].astype(jnp.float32)
    placed_ref[...] = jnp.zeros(placed_ref.shape, jnp.float32)
    total = jnp.zeros(residual.shape, jnp.float32)
    for k in range(parts):
        copies[k].wait()
        for h in range(k * each, (k + 1) * each, 2):
            left, right = (
                jnp.concatenate(pair, axis=1)
                for pair in (
                    [
                        stripes_ref[:, i * span : (i + 1) * span, :].reshape(-1, LANES)
                        for i in (h, h + 1)
                    ],
                    [held[i].reshape(width, LANES) for i in (h, h + 1)],
                )
            )
            total = total + contract_last(left, right)
    mixed = residual + gate_ref[...] * total
    mean = jnp.mean(mixed, axis=1, keepdims=True)
    left, told, columns = mean, jnp.zeros_like(mean), []
    for _ in range(MEAN_PARTS):
        columns.append(left.astype(jnp.bfloat16).astype(jnp.float32))
        told = told + columns[-1]
        left = mean - told
    lane = lax.broadcasted_iota(jnp.int32, (rows, -width % LANES), 1)
    rest = jnp.zeros(lane.shape, jnp.float32)
    for k, column in enumerate(columns):
        rest = jnp.where(lane == k, column, rest)
    rest = jnp.where(lane == 16, told, rest)
    turned = jnp.concatenate([mixed, rest], axis=1).T
    message_ref[0:width, :] = (turned[0:width] - turned[width + 16 : width + 17]).astype(
        jnp.bfloat16
    )
    message_ref[width : width + 16, :] = turned[width : width + 16].astype(jnp.bfloat16)
    at = pl.multiple_of(place_ref[1] * half, half)
    for core in range(CORES):
        placed_ref[core, pl.ds(at, half), :] = turned[core * half : (core + 1) * half]


def project(place, stripes, everything, residual, gate):
    rows, outs = residual.shape
    sp = everything.shape[0]
    parts = 8
    vmem = pl.BlockSpec(memory_space=pltpu.VMEM)
    smem = pl.BlockSpec(memory_space=pltpu.SMEM)
    return pl.pallas_call(
        functools.partial(project_kernel, parts),
        out_shape=(
            jax.ShapeDtypeStruct((CORES, outs, rows), jnp.float32),
            jax.ShapeDtypeStruct((outs + 16, rows), jnp.bfloat16),
        ),
        in_specs=[smem, vmem, pl.BlockSpec(memory_space=pltpu.HBM), vmem, vmem],
        out_specs=(vmem, vmem),
        scratch_shapes=[
            pltpu.VMEM((sp, CORES, outs // CORES, LANES), jnp.bfloat16),
            pltpu.SemaphoreType.DMA((parts,)),
        ],
        compiler_params=pltpu.CompilerParams(vmem_limit_bytes=LIMIT * MEBI),
        name="project",
    )(place, stripes, everything, residual, gate)


def feed_kernel(
    place_ref, messages_ref, scales_ref, gates_ref, placed_ref, weights_ref, shares_ref, ups, downs, sems
):
    _, sp, depth, up_width = ups.shape
    whole = downs.shape[3]
    pieces = whole // LANES
    tp_size, outs, rows = gates_ref.shape
    chips = tp_size // CORES
    half = outs // PAIR
    copies, slot = ([], [], []), 0
    for kind, (first, held, count) in enumerate(
        ((half, ups, pieces), (half + 2 * pieces * depth, ups, 1), (half + pieces * depth, downs, pieces))
    ):
        for core in range(CORES):
            for j in range(count):
                lanes = (pieces if kind == 1 else j) * LANES
                copies[kind].append(
                    pltpu.make_async_copy(
                        weights_ref.at[:, core, pl.ds(first + j * depth, depth), :],
                        held.at[core, :, :, pl.ds(lanes, LANES)],
                        sems.at[slot],
                    )
                )
                slot += 1
    for group in copies:
        for copy in group:
            copy.start()
    spreads = []
    for t in range(tp_size):
        for member in range(PAIR):
            source = member * chips + t // CORES
            mean = jnp.sum(
                messages_ref[source, outs : outs + 16, :].astype(jnp.float32),
                axis=0,
                keepdims=True,
            )
            start = t % CORES * half
            spreads.append(
                messages_ref[source, start : start + half, :].astype(jnp.float32) + mean
            )
    features = tp_size * outs
    row_mean = sum(jnp.sum(part, axis=0, keepdims=True) for part in spreads) / features
    centred = [part - row_mean for part in spreads]
    spread = sum(jnp.sum(part * part, axis=0, keepdims=True) for part in centred) / features
    factor = lax.rsqrt(spread + 1e-06)
    turned = jnp.concatenate([part * factor for part in centred], axis=0).T
    normed = (turned * (1.0 + scales_ref[1:2, :]) + scales_ref[0:1, :]).astype(jnp.bfloat16)
    for copy in [*copies[0], *copies[1]]:
        copy.wait()
    active = []
    for core in range(CORES):
        for start in range(0, up_width, 2 * LANES):
            block = ups[core, :, :, start : start + 2 * LANES].reshape(sp * depth, -1)
            hidden = jnp.dot(normed, block, preferred_element_type=jnp.float32)
            active.append(jax.nn.gelu(hidden, approximate=True))
    lane = lax.broadcasted_iota(jnp.int32, (rows, LANES), 1)
    for core in range(CORES):
        tail = active[2 * core + 1]
        moved = jnp.where(lane < LANES // 2, 0.0, pltpu.roll(tail[:, LANES:], LANES // 2, 1))
        active[2 * core + 1] = jnp.concatenate([tail[:, :LANES], moved], axis=1)
    active = [part.astype(jnp.bfloat16) for part in active]
    for copy in copies[2]:
        copy.wait()
    each = sp // tp_size
    low = lax.broadcasted_iota(jnp.int32, (half, rows), 1) < rows // 2
    for t in range(tp_size):
        total = jnp.zeros((outs, rows), jnp.float32)
        for core in range(CORES):
            block = jnp.concatenate(
                [
                    downs[core, t * each : (t + 1) * each].reshape(each * depth, whole),
                    ups[core, t * each : (t + 1) * each, :, whole:].reshape(each * depth, LANES),
                ],
                axis=1,
            )
            kept = jnp.concatenate([active[2 * core], active[2 * core + 1]], axis=1)
            total = total + contract_last(block, kept)
        total = total * gates_ref[t]
        total = total + jnp.where(place_ref[0] == t // CORES, placed_ref[t % CORES], 0.0)
        top, bottom = total[:half], total[half:]
        shares_ref[0, t] = jnp.where(low, top, pltpu.roll(bottom, rows // 2, 1)).astype(
            jnp.bfloat16
        )
        shares_ref[1, t] = jnp.where(low, pltpu.roll(top, rows // 2, 1), bottom).astype(
            jnp.bfloat16
        )


def feed(place, messages, scales, gates, placed, everything, depth, units):
    tp_size, outs, rows = gates.shape
    sp = everything.shape[0]
    pieces = units // PAIR // LANES
    vmem = pl.BlockSpec(memory_space=pltpu.VMEM)
    smem = pl.BlockSpec(memory_space=pltpu.SMEM)
    return pl.pallas_call(
        feed_kernel,
        out_shape=jax.ShapeDtypeStruct((PAIR, tp_size, outs // PAIR, rows), jnp.bfloat16),
        in_specs=[smem, vmem, vmem, vmem, vmem, pl.BlockSpec(memory_space=pltpu.HBM)],
        out_specs=vmem,
        scratch_shapes=[
            pltpu.VMEM((CORES, sp, depth, (pieces + 1) * LANES), jnp.bfloat16),
            pltpu.VMEM((CORES, sp, depth, pieces * LANES), jnp.bfloat16),
            pltpu.SemaphoreType.DMA((CORES * (2 * pieces + 1),)),
        ],
        compiler_params=pltpu.CompilerParams(vmem_limit_bytes=LIMIT * MEBI),
        name="feed",
    )(place, messages, scales, gates, placed, everything)


def finish_kernel(shares_ref, out_ref):
    sources = shares_ref.shape[0]
    batches, span, _ = out_ref.shape
    for batch in range(batches):
        total = jnp.zeros(shares_ref.shape[1:], jnp.float32)
        for source in range(batch, sources, batches):
            total = total + shares_ref[source].astype(jnp.float32)
        rest = jnp.zeros((-total.shape[0] % LANES, total.shape[1]), jnp.float32)
        turned = jnp.concatenate([total, rest], axis=0).T[:, : total.shape[0]]
        both = jnp.concatenate([turned[k * span : (k + 1) * span] for k in range(PAIR)], axis=1)
        out_ref[batch] = both.astype(jnp.bfloat16)


def body(
    query_rows, key_rows, value_rows, residual, modulation, out_weight, up_weight, down_weight
):
    side, chip = lax.axis_index("member"), lax.axis_index("x")
    everything = gathered_weights(out_weight, up_weight, down_weight, side)
    tp = ("x", "core")
    tp_size = lax.axis_size(tp)
    batches, rows_block, local_width = residual.shape
    depth, units = up_weight.shape
    rows = PAIR * rows_block
    half = local_width // PAIR

    parts = residual.reshape(batches, rows_block, PAIR, half).transpose(2, 0, 1, 3)
    parts = lax.all_to_all(
        parts.reshape(PAIR * batches, rows_block, half), ("member", "core"), 0, 0, tiled=True
    )
    parts = parts.reshape(PAIR, CORES, rows_block, half).transpose(0, 2, 1, 3)
    residual_rows = parts.reshape(rows, CORES * half)
    rows_of_modulation = lax.all_gather(modulation, tp, axis=0, tiled=False)
    scales = jnp.swapaxes(rows_of_modulation[:, 1:3], 0, 1).reshape(2, -1)
    gates = jnp.broadcast_to(
        rows_of_modulation[:, 3][:, :, None], (tp_size, local_width, rows)
    )
    gate = lax.dynamic_slice_in_dim(rows_of_modulation[:, 0], chip * CORES, CORES, axis=0)
    gate = jnp.where(side == 0, gate[:, :half], gate[:, half:]).reshape(1, CORES * half)

    own = attend(query_rows, key_rows, value_rows)
    stripes = sent_to_all(own.reshape(-1, HEAD_FEATURES), ("member", "x"))
    place = jnp.stack([chip, side]).astype(jnp.int32)
    placed, message = project(place, stripes, everything, residual_rows, gate)
    messages = lax.all_gather(message, ("member", "x"), axis=0, tiled=False)
    shares = feed(place, messages, scales, gates, placed, everything, depth, units)
    shares = shares.reshape(PAIR * tp_size, half, rows)
    shares = lax.all_to_all(shares, ("member", "x", "core"), 0, 0, tiled=True)
    return pl.pallas_call(
        finish_kernel,
        out_shape=jax.ShapeDtypeStruct(residual.shape, residual.dtype),
        compiler_params=pltpu.CompilerParams(vmem_limit_bytes=8 * MEBI),
        name="finish",
    )(shares)


def solution(mesh):
    groups, tp, sp = (mesh.shape[a] for a in ("groups", "tp", "sp"))
    fine = Mesh(
        mesh.devices.reshape(groups // PAIR, PAIR, tp // CORES, CORES, sp),
        ("pairs", "member", "x", "core", "sp"),
    )
    jobs, tokens, tensor = ("pairs", "member"), ("sp", "x", "core"), ("x", "core")
    in_specs = (
        P(jobs, tokens, None),
        P(jobs, tokens, None),
        P(jobs, tokens, None),
        P(jobs, "sp", tensor),
        P(None, tensor),
        P(tensor, "sp"),
        P("sp", tensor),
        P("sp", tensor),
    )
    out_specs = P(jobs, "sp", tensor)
    return jax.shard_map(body, mesh=fine, in_specs=in_specs, out_specs=out_specs, check_vma=False)
```

time: 287 us -> 278 us (0.969)
  waiting for transfers between devices: 77.3 us -> 19.8 us
  blocking collectives: 166 us -> 205 us
  starting transfers between devices: 10.3 us -> 16.9 us
    all_to_all x1, waiting for transfers between devices: 30.9 us -> 1.41 us  [body(): lax.all_to_all(parts.reshape(PAIR * batches, rows_block, half), ('member'...]
    all_gather x1, waiting for transfers between devices: 33.8 us -> 7.03 us  [gathered_weights(): everything = lax.all_gather(packed, ('sp', 'core'), axis=0, tiled=False)]
    all_to_all x2, blocking collectives: 36.2 us -> 56.4 us  [the longest x1 36.2 us: attend(): return lax.all_to_all(back, 'sp', split_axis=0, concat_axis=0, tiled=True)]
    all_gather x1 -> x2, blocking collectives: 23.1 us -> 41.9 us  [the longest x1 23 us: body(): rows_of_modulation = lax.all_gather(modulation, tp, axis=0, tiled=False)]
    all_to_all x1 -> x2, starting transfers between devices: 4.42 us -> 7.8 us  [sent_to_all(): return lax.all_to_all(copies, axis, split_axis=0, concat_axis=0, tiled=True)]
    all_to_all x1, starting transfers between devices: 5.86 us -> 9.12 us  [body(): lax.all_to_all(parts.reshape(PAIR * batches, rows_block, half), ('member'...]
    all_to_all x1 -> x2, waiting for transfers between devices: 12.6 us -> 11.3 us  [sent_to_all(): return lax.all_to_all(copies, axis, split_axis=0, concat_axis=0, tiled=True)]
  transfers between devices with their start and end apart: 3 -> 4, of which waited for: 3 -> 3; matrix products, arithmetic and copies ran while one was open for 2% -> 3% of each run, Pallas kernels for 0% -> 0%
where the time goes in v5:
time: 278 us; the launch traced here: 277 us
  blocking collectives  205 us (74%)
  waiting for transfers between devices  19.8 us (7%)
  starting transfers between devices  16.9 us (6%)
  between operations  13.7 us (5%)
  Pallas kernels  10.4 us (4%)
  local copies, waits for them, and re-layouts  6.97 us (3%)
  other arithmetic  3.05 us (1%)
    all_to_all x1, blocking collectives, attend(): lax.all_to_all(to_heads, 'sp', split_axis=0, concat_axis=0, tiled=True)  61.6 us
    all_to_all x1, blocking collectives, attend(): lax.all_to_all(both, 'core', split_axis=0, concat_axis=0, tiled=True)  45.1 us
    all_to_all x1, blocking collectives, attend(): return lax.all_to_all(back, 'sp', split_axis=0, concat_axis=0, tiled=True)  36.2 us
    all_gather x1, blocking collectives, body(): rows_of_modulation = lax.all_gather(modulation, tp, axis=0, tiled=False)  23 us
    all_to_all x1, blocking collectives, body(): shares = lax.all_to_all(shares, ('member', 'x', 'core'), 0, 0, tiled=True)  20.2 us
    all_gather x1, blocking collectives, body(): messages = lax.all_gather(message, ('member', 'x'), axis=0, tiled=False)  18.9 us
    all_to_all x2, waiting for transfers between devices, sent_to_all(): return lax.all_to_all(copies, axis, split_axis=0, concat_axis=0, tiled=True)  11.3 us
    all_to_all x1, starting transfers between devices, body(): lax.all_to_all(parts.reshape(PAIR * batches, rows_block, half), ('member'...  9.12 us
  transfers between devices with their start and end apart: 4, of which 3 were waited for; matrix products, arithmetic and copies ran while one was open for 3% of the time, Pallas kernels for 0%

profile of v5, /device:TPU:33, one launch (start us, length us, event | category | flops | bytes accessed | tf_op | source)
XLA Modules:
  0.0 277.4 jit_solution(8763049843873506624)
XLA Ops:
  6.5 0.0 all-gather.6.cloned.1.call-start
  6.6 0.8 select_dynamic-update-slice_fusion
  7.4 1.1 slice_select_fusion
  8.6 0.1 maximum_dynamic-update-slice_fusion
  8.7 0.0 copy-start
  8.7 0.7 copy-done
  9.4 0.1 all-gather.6.cloned.1.call-update
  9.5 0.9 copy.35
  10.4 1.0 copy_bitcast_fusion
  11.4 0.0 copy-start.1
  11.5 45.1 %all_to_all.35 = bf16[2,32,3,8,128]{4,1,3,2,0:T(8,128)(2,1)S(1)} all-to-all(bf16[2,32,3,8,128]{4,1,3,2,0:T(8,128)(2,1)S(1)} %copy.18), channel_id=1, replica_groups=mesh['pairs'=1,'member'=2,'x'=4,'core'=2,'sp'=32] {'core'}, dimensions={0} | all-to-all | bytes 786432 | tf_op jit(solution)/shard_map/all_to_all | solution.py:58
  56.6 0.2 copy.19
  56.8 61.6 %all_to_all.36 = bf16[32,48,128]{2,1,0:T(8,128)(2,1)S(1)} all-to-all(bf16[32,48,128]{2,1,0:T(8,128)(2,1)S(1)} %bitcast.62), channel_id=1, replica_groups=mesh['pairs'=1,'member'=2,'x'=4,'core'=2,'sp'=32] {'sp'}, dimensions={0} | all-to-all | bytes 786432 | tf_op jit(solution)/shard_map/all_to_all | solution.py:60
  118.4 1.1 broadcast_in_dim.15
  119.6 4.0 %all-to-all-start.2 = ((bf16[4,2,512,128]{3,2,1,0:T(8,128)(2,1)}), bf16[4,2,512,128]{3,2,1,0:T(8,128)(2,1)S(1)}, u32[]{:S(2)}, u32[]{:S(2)}) async-start(bf16[4,2,512,128]{3,2,1,0:T(8,128)(2,1)} %broadcast_in_dim.15), calls=%async_computation.2 | async-start | bytes 2097152 | tf_op jit(solution)/shard_map/all_to_all | solution.py:28
  123.6 0.0 copy-done.1
  123.6 0.1 reshape.56
  123.7 0.7 copy.21
  124.4 11.3 %all-to-all-done.2 = bf16[4,2,512,128]{3,2,1,0:T(8,128)(2,1)S(1)} async-done(((bf16[4,2,512,128]{3,2,1,0:T(8,128)(2,1)}), bf16[4,2,512,128]{3,2,1,0:T(8,128)(2,1)S(1)}, u32[]{:S(2)}, u32[]{:S(2)}) %all-to-all-start.2) | async-done | bytes 1048608 | tf_op jit(solution)/shard_map/all_to_all | solution.py:28
  135.7 9.1 %all-to-all-start.5 = ((bf16[4,64,160]{2,1,0:T(8,128)(2,1)}), bf16[4,64,160]{2,1,0:T(8,128)(2,1)S(1)}, u32[]{:S(2)}, u32[]{:S(2)}) async-start(bf16[4,64,160]{2,1,0:T(8,128)(2,1)} %bitcast.15), calls=%async_computation.5 | async-start | bytes 262144 | tf_op jit(solution)/shard_map/all_to_all | solution.py:295
  144.8 0.1 fusion.13
  144.9 0.8 multiply_reduce_fusion
  145.6 0.8 fusion
  146.5 0.0 copy-start.2
  146.5 0.8 fusion.9
  147.3 1.4 all-to-all-done.5
  148.8 36.2 %all_to_all.37 = bf16[32,16,128]{2,1,0:T(8,128)(2,1)S(1)} all-to-all(bf16[32,16,128]{2,1,0:T(8,128)(2,1)S(1)} %bitcast.71), channel_id=1, replica_groups=mesh['pairs'=1,'member'=2,'x'=4,'core'=2,'sp'=32] {'sp'}, dimensions={0} | all-to-all | bytes 262144 | tf_op jit(solution)/shard_map/all_to_all | solution.py:76
  184.9 1.1 broadcast_in_dim.16
  186.1 3.8 %all-to-all-start.4 = ((bf16[8,512,128]{2,1,0:T(8,128)(2,1)}), bf16[8,512,128]{2,1,0:T(8,128)(2,1)S(1)}, u32[]{:S(2)}, u32[]{:S(2)}) async-start(bf16[8,512,128]{2,1,0:T(8,128)(2,1)} %broadcast_in_dim.16), calls=%async_computation.4 | async-start | bytes 2097152 | tf_op jit(solution)/shard_map/all_to_all | solution.py:28
  189.8 0.0 copy-done.2
  189.9 23.0 %all-gather.3 = f32[8,4,320]{2,1,0:T(4,128)S(1)} all-gather(f32[1,4,320]{2,1,0:T(4,128)S(1)} %bitcast.76), channel_id=3, replica_groups=mesh['pairs'=1,'member'=2,'x'=4,'core'=2,'sp'=32] {'x','core'}, dimensions={0}, use_global_device_ids=true | all-gather | bytes 46080 | tf_op jit(solution)/shard_map/all_gather | solution.py:300
  212.9 0.1 slice_select_fusion.2
  213.0 0.1 reshape.60.gate_ref
  213.1 0.1 reshape.61.scales_ref
  213.2 0.1 pad_add_fusion.place_ref
  213.3 0.1 copy.22
  213.4 0.1 reshape.59.residual_ref
  213.5 0.0 all-to-all-done.4.stripes_ref
  213.5 7.0 %all-gather.6.cloned.1.call-done = bf16[46080,128]{1,0:T(8,128)(2,1)} async-done(((bf16[720,128]{1,0:T(8,128)(2,1)}), bf16[46080,128]{1,0:T(8,128)(2,1)}) %all-gather.6.cloned.1.call-update) | async-done | bytes 11796496 | tf_op jit(solution)/shard_map/all_gather | solution.py:48
  220.6 3.6 %project.1 = (f32[2,320,128]{2,1,0:T(8,128)S(1)}, bf16[336,128]{1,0:T(8,128)(2,1)S(1)}) custom-call(s32[2]{0:T(128)S(1)} %pad_add_fusion.place_ref, bf16[8,512,128]{2,1,0:T(8,128)(2,1)S(1)} %all-to-all-done.4.stripes_ref, bf16[32,2,720,128]{3,2,1,0:T(8,128)(2,1)} %bitcast.57, bf16[128,320]{1,0:T(8,128)(2,1)S(1)} %reshape.59.residual_ref, ...), custom_call_target="tpu_custom_call" | custom-call | tf_op jit(solution)/shard_map/project/pallas_call | solution.py:143
  224.1 18.9 %all-gather.2 = bf16[2688,128]{1,0:T(8,128)(2,1)S(1)} all-gather(bf16[336,128]{1,0:T(8,128)(2,1)S(1)} %get-tuple-element.7), channel_id=4, replica_groups=mesh['pairs'=1,'member'=2,'x'=4,'core'=2,'sp'=32] {'member','x'}, dimensions={0}, use_global_device_ids=true | all-gather | bytes 774144 | tf_op jit(solution)/shard_map/all_gather | solution.py:312
  243.1 0.4 broadcast_in_dim.18.gates_ref
  243.5 5.9 %feed.1 = bf16[2,8,160,128]{3,2,1,0:T(8,128)(2,1)S(1)} custom-call(s32[2]{0:T(128)S(1)} %pad_add_fusion.place_ref, bf16[8,336,128]{2,1,0:T(8,128)(2,1)S(1)} %bitcast.55, f32[2,2560]{1,0:T(2,128)S(1)} %reshape.61.scales_ref, f32[8,320,128]{2,1,0:T(8,128)S(1)} %broadcast_in_dim.18.gates_ref, f32[2,320,128]{2,1,0:T(8,128)S(1)} %get-tuple-element.8.placed_ref, ...), custom_call_target="tpu_custom_call" | custom-call | tf_op jit(solution)/shard_map/feed/pallas_call | solution.py:254
  249.4 20.2 %all_to_all.38.shares_ref = bf16[16,160,128]{2,1,0:T(8,128)(2,1)S(1)} all-to-all(bf16[16,160,128]{2,1,0:T(8,128)(2,1)S(1)} %bitcast.56), channel_id=1, replica_groups=mesh['pairs'=1,'member'=2,'x'=4,'core'=2,'sp'=32] {'member','x','core'}, dimensions={0} | all-to-all | bytes 1310720 | tf_op jit(solution)/shard_map/all_to_all | solution.py:315
  269.6 0.9 finish.1
  (19 shorter events, 0.3 us)
Async XLA Ops:
  6.5 214.0 %all-gather.6.cloned.1.call-start = ((), (), s32[]{:S(2)}) async-start(), calls=%async_computation.7 | async-start | bytes 11980800 | tf_op jit(solution)/shard_map/all_gather | solution.py:48
  8.7 0.7 copy-start
  11.4 112.2 %copy-start.1 = (bf16[2,64,320]{2,1,0:T(8,128)(2,1)S(1)}, bf16[2,64,320]{2,1,0:T(8,128)(2,1)}, u32[]{:S(2)}) copy-start(bf16[2,64,320]{2,1,0:T(8,128)(2,1)} %param.11) | copy-start | bytes 245764
  119.6 16.1 %all-to-all-start.2 = ((bf16[4,2,512,128]{3,2,1,0:T(8,128)(2,1)}), bf16[4,2,512,128]{3,2,1,0:T(8,128)(2,1)S(1)}, u32[]{:S(2)}, u32[]{:S(2)}) async-start(bf16[4,2,512,128]{3,2,1,0:T(8,128)(2,1)} %broadcast_in_dim.15), calls=%async_computation.2 | async-start | bytes 2097152 | tf_op jit(solution)/shard_map/all_to_all | solution.py:28
  135.7 13.1 %all-to-all-start.5 = ((bf16[4,64,160]{2,1,0:T(8,128)(2,1)}), bf16[4,64,160]{2,1,0:T(8,128)(2,1)S(1)}, u32[]{:S(2)}, u32[]{:S(2)}) async-start(bf16[4,64,160]{2,1,0:T(8,128)(2,1)} %bitcast.15), calls=%async_computation.5 | async-start | bytes 262144 | tf_op jit(solution)/shard_map/all_to_all | solution.py:295
  146.5 43.4 %copy-start.2 = (f32[4,320]{1,0:T(4,128)S(1)}, f32[4,320]{1,0:T(4,128)}, u32[]{:S(2)}) copy-start(f32[4,320]{1,0:T(4,128)} %param.12) | copy-start | bytes 15364
  186.1 27.4 %all-to-all-start.4 = ((bf16[8,512,128]{2,1,0:T(8,128)(2,1)}), bf16[8,512,128]{2,1,0:T(8,128)(2,1)S(1)}, u32[]{:S(2)}, u32[]{:S(2)}) async-start(bf16[8,512,128]{2,1,0:T(8,128)(2,1)} %broadcast_in_dim.16), calls=%async_computation.4 | async-start | bytes 2097152 | tf_op jit(solution)/shard_map/all_to_all | solution.py:28
Sparse Core Ops, SparseCore 0:
  9.6 210.9 all-gather.5

commit v6 on v5

--- a/solution.py
+++ b/solution.py
@@ -125,10 +125,11 @@
         rest = jnp.where(lane == k, column, rest)
     rest = jnp.where(lane == 16, told, rest)
     turned = jnp.concatenate([mixed, rest], axis=1).T
-    message_ref[0:width, :] = (turned[0:width] - turned[width + 16 : width + 17]).astype(
-        jnp.bfloat16
-    )
-    message_ref[width : width + 16, :] = turned[width : width + 16].astype(jnp.bfloat16)
+    deviation = (turned[0:width] - turned[width + 16 : width + 17]).astype(jnp.bfloat16)
+    means = turned[width : width + 16].astype(jnp.bfloat16)
+    for k in range(message_ref.shape[0]):
+        message_ref[k, 0:width, :] = deviation
+        message_ref[k, width : width + 16, :] = means
     at = pl.multiple_of(place_ref[1] * half, half)
     for core in range(CORES):
         placed_ref[core, pl.ds(at, half), :] = turned[core * half : (core + 1) * half]
@@ -144,7 +145,7 @@
         functools.partial(project_kernel, parts),
         out_shape=(
             jax.ShapeDtypeStruct((CORES, outs, rows), jnp.float32),
-            jax.ShapeDtypeStruct((outs + 16, rows), jnp.bfloat16),
+            jax.ShapeDtypeStruct((stripes.shape[0], outs + 16, rows), jnp.bfloat16),
         ),
         in_specs=[smem, vmem, pl.BlockSpec(memory_space=pltpu.HBM), vmem, vmem],
         out_specs=(vmem, vmem),
@@ -308,8 +309,9 @@
     own = attend(query_rows, key_rows, value_rows)
     stripes = sent_to_all(own.reshape(-1, HEAD_FEATURES), ("member", "x"))
     place = jnp.stack([chip, side]).astype(jnp.int32)
-    placed, message = project(place, stripes, everything, residual_rows, gate)
-    messages = lax.all_gather(message, ("member", "x"), axis=0, tiled=False)
+    stripes, gates = lax.optimization_barrier((stripes, gates))
+    placed, messages = project(place, stripes, everything, residual_rows, gate)
+    messages = lax.all_to_all(messages, ("member", "x"), 0, 0, tiled=True)
     shares = feed(place, messages, scales, gates, placed, everything, depth, units)
     shares = shares.reshape(PAIR * tp_size, half, rows)
     shares = lax.all_to_all(shares, ("member", "x", "core"), 0, 0, tiled=True)

time: 278 us -> 271 us (0.975)
  blocking collectives: 205 us -> 182 us
  waiting for transfers between devices: 19.8 us -> 30.8 us
  starting transfers between devices: 16.9 us -> 21.6 us
    all_gather x1 -> x0, blocking collectives: 18.9 us -> none  [body(): messages = lax.all_gather(message, ('member', 'x'), axis=0, tiled=False)]
    all_to_all x0 -> x1, waiting for transfers between devices: none -> 10.5 us  [body(): messages = lax.all_to_all(messages, ('member', 'x'), 0, 0, tiled=True)]
    all_to_all x0 -> x1, starting transfers between devices: none -> 4.64 us  [body(): messages = lax.all_to_all(messages, ('member', 'x'), 0, 0, tiled=True)]
    all_to_all x1, blocking collectives: 20.2 us -> 16.5 us  [body(): shares = lax.all_to_all(shares, ('member', 'x', 'core'), 0, 0, tiled=True)]
  transfers between devices with their start and end apart: 4 -> 5, of which waited for: 3 -> 4; matrix products, arithmetic and copies ran while one was open for 3% -> 3% of each run, Pallas kernels for 0% -> 0%
where the time goes in v6:
time: 271 us; the launch traced here: 270 us
  blocking collectives  182 us (67%)
  waiting for transfers between devices  30.8 us (11%)
  starting transfers between devices  21.6 us (8%)
  between operations  13.7 us (5%)
  Pallas kernels  11.2 us (4%)
  local copies, waits for them, and re-layouts  6.98 us (3%)
  other arithmetic  3.04 us (1%)
    all_to_all x1, blocking collectives, attend(): lax.all_to_all(to_heads, 'sp', split_axis=0, concat_axis=0, tiled=True)  61.6 us
    all_to_all x1, blocking collectives, attend(): lax.all_to_all(both, 'core', split_axis=0, concat_axis=0, tiled=True)  45.1 us
    all_to_all x1, blocking collectives, attend(): return lax.all_to_all(back, 'sp', split_axis=0, concat_axis=0, tiled=True)  35.4 us
    all_gather x1, blocking collectives, body(): rows_of_modulation = lax.all_gather(modulation, tp, axis=0, tiled=False)  23 us
    all_to_all x1, blocking collectives, body(): shares = lax.all_to_all(shares, ('member', 'x', 'core'), 0, 0, tiled=True)  16.5 us
    all_to_all x2, waiting for transfers between devices, sent_to_all(): return lax.all_to_all(copies, axis, split_axis=0, concat_axis=0, tiled=True)  11.2 us
    all_to_all x1, waiting for transfers between devices, body(): messages = lax.all_to_all(messages, ('member', 'x'), 0, 0, tiled=True)  10.5 us
    all_to_all x1, starting transfers between devices, body(): lax.all_to_all(parts.reshape(PAIR * batches, rows_block, half), ('member'...  9.14 us
  transfers between devices with their start and end apart: 5, of which 4 were waited for; matrix products, arithmetic and copies ran while one was open for 3% of the time, Pallas kernels for 0%

profile of v6, /device:TPU:33, one launch (start us, length us, event | category | flops | bytes accessed | tf_op | source)
XLA Modules:
  0.0 270.5 jit_solution(5900193991244257329)
XLA Ops:
  6.5 0.0 all-gather.5.cloned.1.call-start
  6.6 0.8 select_dynamic-update-slice_fusion
  7.4 1.1 slice_select_fusion
  8.6 0.1 maximum_dynamic-update-slice_fusion
  8.7 0.0 copy-start
  8.7 0.7 copy-done
  9.4 0.1 all-gather.5.cloned.1.call-update
  9.5 0.9 copy.35
  10.4 1.0 copy_bitcast_fusion
  11.4 0.0 copy-start.1
  11.5 45.1 %all_to_all.40 = bf16[2,32,3,8,128]{4,1,3,2,0:T(8,128)(2,1)S(1)} all-to-all(bf16[2,32,3,8,128]{4,1,3,2,0:T(8,128)(2,1)S(1)} %copy.18), channel_id=1, replica_groups=mesh['pairs'=1,'member'=2,'x'=4,'core'=2,'sp'=32] {'core'}, dimensions={0} | all-to-all | bytes 786432 | tf_op jit(solution)/shard_map/all_to_all | solution.py:58
  56.6 0.2 copy.19
  56.8 61.6 %all_to_all.41 = bf16[32,48,128]{2,1,0:T(8,128)(2,1)S(1)} all-to-all(bf16[32,48,128]{2,1,0:T(8,128)(2,1)S(1)} %bitcast.60), channel_id=1, replica_groups=mesh['pairs'=1,'member'=2,'x'=4,'core'=2,'sp'=32] {'sp'}, dimensions={0} | all-to-all | bytes 786432 | tf_op jit(solution)/shard_map/all_to_all | solution.py:60
  118.4 1.2 broadcast_in_dim.15
  119.6 4.0 %all-to-all-start.2 = ((bf16[4,2,512,128]{3,2,1,0:T(8,128)(2,1)}), bf16[4,2,512,128]{3,2,1,0:T(8,128)(2,1)S(1)}, u32[]{:S(2)}, u32[]{:S(2)}) async-start(bf16[4,2,512,128]{3,2,1,0:T(8,128)(2,1)} %broadcast_in_dim.15), calls=%async_computation.2 | async-start | bytes 2097152 | tf_op jit(solution)/shard_map/all_to_all | solution.py:28
  123.6 0.0 copy-done.1
  123.6 0.1 reshape.56
  123.7 0.7 copy.21
  124.4 11.2 %all-to-all-done.2 = bf16[4,2,512,128]{3,2,1,0:T(8,128)(2,1)S(1)} async-done(((bf16[4,2,512,128]{3,2,1,0:T(8,128)(2,1)}), bf16[4,2,512,128]{3,2,1,0:T(8,128)(2,1)S(1)}, u32[]{:S(2)}, u32[]{:S(2)}) %all-to-all-start.2) | async-done | bytes 1048608 | tf_op jit(solution)/shard_map/all_to_all | solution.py:28
  135.7 9.1 %all-to-all-start.5 = ((bf16[4,64,160]{2,1,0:T(8,128)(2,1)}), bf16[4,64,160]{2,1,0:T(8,128)(2,1)S(1)}, u32[]{:S(2)}, u32[]{:S(2)}) async-start(bf16[4,64,160]{2,1,0:T(8,128)(2,1)} %bitcast.16), calls=%async_computation.5 | async-start | bytes 262144 | tf_op jit(solution)/shard_map/all_to_all | solution.py:296
  144.8 0.1 fusion.13
  144.9 0.8 multiply_reduce_fusion
  145.7 0.8 fusion
  146.5 0.0 copy-start.2
  146.5 0.8 fusion.9
  147.3 1.4 all-to-all-done.5
  148.8 35.4 %all_to_all.42 = bf16[32,16,128]{2,1,0:T(8,128)(2,1)S(1)} all-to-all(bf16[32,16,128]{2,1,0:T(8,128)(2,1)S(1)} %bitcast.69), channel_id=1, replica_groups=mesh['pairs'=1,'member'=2,'x'=4,'core'=2,'sp'=32] {'sp'}, dimensions={0} | all-to-all | bytes 262144 | tf_op jit(solution)/shard_map/all_to_all | solution.py:76
  184.2 1.1 broadcast_in_dim.16
  185.3 3.8 %all-to-all-start.4 = ((bf16[8,512,128]{2,1,0:T(8,128)(2,1)}), bf16[8,512,128]{2,1,0:T(8,128)(2,1)S(1)}, u32[]{:S(2)}, u32[]{:S(2)}) async-start(bf16[8,512,128]{2,1,0:T(8,128)(2,1)} %broadcast_in_dim.16), calls=%async_computation.4 | async-start | bytes 2097152 | tf_op jit(solution)/shard_map/all_to_all | solution.py:28
  189.1 0.0 copy-done.2
  189.1 23.0 %all-gather.2 = f32[8,4,320]{2,1,0:T(4,128)S(1)} all-gather(f32[1,4,320]{2,1,0:T(4,128)S(1)} %bitcast.74), channel_id=2, replica_groups=mesh['pairs'=1,'member'=2,'x'=4,'core'=2,'sp'=32] {'x','core'}, dimensions={0}, use_global_device_ids=true | all-gather | bytes 46080 | tf_op jit(solution)/shard_map/all_gather | solution.py:301
  212.1 0.1 slice_select_fusion.2
  212.2 0.1 reshape.60.gate_ref
  212.3 0.1 pad_add_fusion.place_ref
  212.4 0.1 copy.22
  212.5 0.1 reshape.59.residual_ref
  212.6 0.0 all-to-all-done.4.stripes_ref
  212.7 0.4 broadcast_in_dim.18.gates_ref
  213.1 7.6 %all-gather.5.cloned.1.call-done = bf16[46080,128]{1,0:T(8,128)(2,1)} async-done(((bf16[720,128]{1,0:T(8,128)(2,1)}), bf16[46080,128]{1,0:T(8,128)(2,1)}) %all-gather.5.cloned.1.call-update) | async-done | bytes 11796496 | tf_op jit(solution)/shard_map/all_gather | solution.py:48
  220.6 4.5 %project.1 = (f32[2,320,128]{2,1,0:T(8,128)S(1)}, bf16[8,336,128]{2,1,0:T(8,128)(2,1)}) custom-call(s32[2]{0:T(128)S(1)} %pad_add_fusion.place_ref, bf16[8,512,128]{2,1,0:T(8,128)(2,1)S(1)} %all-to-all-done.4.stripes_ref, bf16[32,2,720,128]{3,2,1,0:T(8,128)(2,1)} %bitcast.55, bf16[128,320]{1,0:T(8,128)(2,1)S(1)} %reshape.59.residual_ref, ...), custom_call_target="tpu_custom_call" | custom-call | tf_op jit(solution)/shard_map/project/pallas_call | solution.py:144
  225.1 4.6 %all-to-all-start.6 = ((bf16[8,336,128]{2,1,0:T(8,128)(2,1)}), bf16[8,336,128]{2,1,0:T(8,128)(2,1)S(1)}, u32[]{:S(2)}, u32[]{:S(2)}) async-start(bf16[8,336,128]{2,1,0:T(8,128)(2,1)} %get-tuple-element.10), calls=%async_computation.6 | async-start | bytes 1376256 | tf_op jit(solution)/shard_map/all_to_all | solution.py:314
  229.8 0.1 reshape.61.scales_ref
  229.9 10.5 %all-to-all-done.6.messages_ref = bf16[8,336,128]{2,1,0:T(8,128)(2,1)S(1)} async-done(((bf16[8,336,128]{2,1,0:T(8,128)(2,1)}), bf16[8,336,128]{2,1,0:T(8,128)(2,1)S(1)}, u32[]{:S(2)}, u32[]{:S(2)}) %all-to-all-start.6) | async-done | bytes 688160 | tf_op jit(solution)/shard_map/all_to_all | solution.py:314
  240.4 5.9 %feed.1 = bf16[2,8,160,128]{3,2,1,0:T(8,128)(2,1)S(1)} custom-call(s32[2]{0:T(128)S(1)} %pad_add_fusion.place_ref, bf16[8,336,128]{2,1,0:T(8,128)(2,1)S(1)} %all-to-all-done.6.messages_ref, f32[2,2560]{1,0:T(2,128)S(1)} %reshape.61.scales_ref, f32[8,320,128]{2,1,0:T(8,128)S(1)} %broadcast_in_dim.18.gates_ref, ...), custom_call_target="tpu_custom_call" | custom-call | tf_op jit(solution)/shard_map/feed/pallas_call | solution.py:255
  246.3 16.5 %all_to_all.43.shares_ref = bf16[16,160,128]{2,1,0:T(8,128)(2,1)S(1)} all-to-all(bf16[16,160,128]{2,1,0:T(8,128)(2,1)S(1)} %bitcast.54), channel_id=1, replica_groups=mesh['pairs'=1,'member'=2,'x'=4,'core'=2,'sp'=32] {'member','x','core'}, dimensions={0} | all-to-all | bytes 1310720 | tf_op jit(solution)/shard_map/all_to_all | solution.py:317
  262.7 0.9 finish.1
  (19 shorter events, 0.3 us)
Async XLA Ops:
  6.5 214.1 %all-gather.5.cloned.1.call-start = ((), (), s32[]{:S(2)}) async-start(), calls=%async_computation.8 | async-start | bytes 11980800 | tf_op jit(solution)/shard_map/all_gather | solution.py:48
  8.7 0.7 copy-start
  11.4 112.2 %copy-start.1 = (bf16[2,64,320]{2,1,0:T(8,128)(2,1)S(1)}, bf16[2,64,320]{2,1,0:T(8,128)(2,1)}, u32[]{:S(2)}) copy-start(bf16[2,64,320]{2,1,0:T(8,128)(2,1)} %param.11) | copy-start | bytes 245764
  119.6 16.1 %all-to-all-start.2 = ((bf16[4,2,512,128]{3,2,1,0:T(8,128)(2,1)}), bf16[4,2,512,128]{3,2,1,0:T(8,128)(2,1)S(1)}, u32[]{:S(2)}, u32[]{:S(2)}) async-start(bf16[4,2,512,128]{3,2,1,0:T(8,128)(2,1)} %broadcast_in_dim.15), calls=%async_computation.2 | async-start | bytes 2097152 | tf_op jit(solution)/shard_map/all_to_all | solution.py:28
  135.7 13.1 %all-to-all-start.5 = ((bf16[4,64,160]{2,1,0:T(8,128)(2,1)}), bf16[4,64,160]{2,1,0:T(8,128)(2,1)S(1)}, u32[]{:S(2)}, u32[]{:S(2)}) async-start(bf16[4,64,160]{2,1,0:T(8,128)(2,1)} %bitcast.16), calls=%async_computation.5 | async-start | bytes 262144 | tf_op jit(solution)/shard_map/all_to_all | solution.py:296
  146.5 42.6 %copy-start.2 = (f32[4,320]{1,0:T(4,128)S(1)}, f32[4,320]{1,0:T(4,128)}, u32[]{:S(2)}) copy-start(f32[4,320]{1,0:T(4,128)} %param.12) | copy-start | bytes 15364
  185.3 27.3 %all-to-all-start.4 = ((bf16[8,512,128]{2,1,0:T(8,128)(2,1)}), bf16[8,512,128]{2,1,0:T(8,128)(2,1)S(1)}, u32[]{:S(2)}, u32[]{:S(2)}) async-start(bf16[8,512,128]{2,1,0:T(8,128)(2,1)} %broadcast_in_dim.16), calls=%async_computation.4 | async-start | bytes 2097152 | tf_op jit(solution)/shard_map/all_to_all | solution.py:28
  225.1 15.2 %all-to-all-start.6 = ((bf16[8,336,128]{2,1,0:T(8,128)(2,1)}), bf16[8,336,128]{2,1,0:T(8,128)(2,1)S(1)}, u32[]{:S(2)}, u32[]{:S(2)}) async-start(bf16[8,336,128]{2,1,0:T(8,128)(2,1)} %get-tuple-element.10), calls=%async_computation.6 | async-start | bytes 1376256 | tf_op jit(solution)/shard_map/all_to_all | solution.py:314
Sparse Core Ops, SparseCore 0:
  9.6 211.0 all-gather.4

commit v7 on v6

--- a/solution.py
+++ b/solution.py
@@ -182,9 +182,11 @@
                     )
                 )
                 slot += 1
-    for group in copies:
-        for copy in group:
-            copy.start()
+    ordered = []
+    for core in range(CORES):
+        ordered += [*copies[0][core * pieces : (core + 1) * pieces], copies[1][core]]
+    for copy in [*ordered, *copies[2]]:
+        copy.start()
     spreads = []
     for t in range(tp_size):
         for member in range(PAIR):
@@ -205,11 +207,12 @@
     factor = lax.rsqrt(spread + 1e-06)
     turned = jnp.concatenate([part * factor for part in centred], axis=0).T
     normed = (turned * (1.0 + scales_ref[1:2, :]) + scales_ref[0:1, :]).astype(jnp.bfloat16)
-    for copy in [*copies[0], *copies[1]]:
-        copy.wait()
     active = []
     for core in range(CORES):
         for start in range(0, up_width, 2 * LANES):
+            first = core * (pieces + 1) + start // LANES
+            for copy in ordered[first : first + 2]:
+                copy.wait()
             block = ups[core, :, :, start : start + 2 * LANES].reshape(sp * depth, -1)
             hidden = jnp.dot(normed, block, preferred_element_type=jnp.float32)
             active.append(jax.nn.gelu(hidden, approximate=True))

time: 271 us -> 271 us (level)
  no operation moved by 1% of the time
where the time goes in v7:
time: 271 us; the launch traced here: 270 us
  blocking collectives  182 us (67%)
  waiting for transfers between devices  30.8 us (11%)
  starting transfers between devices  21.6 us (8%)
  between operations  13.7 us (5%)
  Pallas kernels  11.2 us (4%)
  local copies, waits for them, and re-layouts  6.98 us (3%)
  other arithmetic  3.04 us (1%)
    all_to_all x1, blocking collectives, attend(): lax.all_to_all(to_heads, 'sp', split_axis=0, concat_axis=0, tiled=True)  61.6 us
    all_to_all x1, blocking collectives, attend(): lax.all_to_all(both, 'core', split_axis=0, concat_axis=0, tiled=True)  45.1 us
    all_to_all x1, blocking collectives, attend(): return lax.all_to_all(back, 'sp', split_axis=0, concat_axis=0, tiled=True)  35.4 us
    all_gather x1, blocking collectives, body(): rows_of_modulation = lax.all_gather(modulation, tp, axis=0, tiled=False)  23 us
    all_to_all x1, blocking collectives, body(): shares = lax.all_to_all(shares, ('member', 'x', 'core'), 0, 0, tiled=True)  16.5 us
    all_to_all x2, waiting for transfers between devices, sent_to_all(): return lax.all_to_all(copies, axis, split_axis=0, concat_axis=0, tiled=True)  11.2 us
    all_to_all x1, waiting for transfers between devices, body(): messages = lax.all_to_all(messages, ('member', 'x'), 0, 0, tiled=True)  10.5 us
    all_to_all x1, starting transfers between devices, body(): lax.all_to_all(parts.reshape(PAIR * batches, rows_block, half), ('member'...  9.14 us
  transfers between devices with their start and end apart: 5, of which 4 were waited for; matrix products, arithmetic and copies ran while one was open for 3% of the time, Pallas kernels for 0%

profile of v7, /device:TPU:33, one launch (start us, length us, event | category | flops | bytes accessed | tf_op | source)
XLA Modules:
  0.0 270.5 jit_solution(14471622494206297211)
XLA Ops:
  6.5 0.0 all-gather.5.cloned.1.call-start
  6.6 0.8 select_dynamic-update-slice_fusion
  7.4 1.1 slice_select_fusion
  8.6 0.1 maximum_dynamic-update-slice_fusion
  8.7 0.0 copy-start
  8.7 0.7 copy-done
  9.4 0.1 all-gather.5.cloned.1.call-update
  9.5 0.9 copy.35
  10.4 1.0 copy_bitcast_fusion
  11.4 0.0 copy-start.1
  11.5 45.1 %all_to_all.40 = bf16[2,32,3,8,128]{4,1,3,2,0:T(8,128)(2,1)S(1)} all-to-all(bf16[2,32,3,8,128]{4,1,3,2,0:T(8,128)(2,1)S(1)} %copy.18), channel_id=1, replica_groups=mesh['pairs'=1,'member'=2,'x'=4,'core'=2,'sp'=32] {'core'}, dimensions={0} | all-to-all | bytes 786432 | tf_op jit(solution)/shard_map/all_to_all | solution.py:58
  56.6 0.2 copy.19
  56.8 61.6 %all_to_all.41 = bf16[32,48,128]{2,1,0:T(8,128)(2,1)S(1)} all-to-all(bf16[32,48,128]{2,1,0:T(8,128)(2,1)S(1)} %bitcast.60), channel_id=1, replica_groups=mesh['pairs'=1,'member'=2,'x'=4,'core'=2,'sp'=32] {'sp'}, dimensions={0} | all-to-all | bytes 786432 | tf_op jit(solution)/shard_map/all_to_all | solution.py:60
  118.4 1.2 broadcast_in_dim.15
  119.6 4.0 %all-to-all-start.2 = ((bf16[4,2,512,128]{3,2,1,0:T(8,128)(2,1)}), bf16[4,2,512,128]{3,2,1,0:T(8,128)(2,1)S(1)}, u32[]{:S(2)}, u32[]{:S(2)}) async-start(bf16[4,2,512,128]{3,2,1,0:T(8,128)(2,1)} %broadcast_in_dim.15), calls=%async_computation.2 | async-start | bytes 2097152 | tf_op jit(solution)/shard_map/all_to_all | solution.py:28
  123.6 0.0 copy-done.1
  123.6 0.1 reshape.56
  123.7 0.7 copy.21
  124.4 11.2 %all-to-all-done.2 = bf16[4,2,512,128]{3,2,1,0:T(8,128)(2,1)S(1)} async-done(((bf16[4,2,512,128]{3,2,1,0:T(8,128)(2,1)}), bf16[4,2,512,128]{3,2,1,0:T(8,128)(2,1)S(1)}, u32[]{:S(2)}, u32[]{:S(2)}) %all-to-all-start.2) | async-done | bytes 1048608 | tf_op jit(solution)/shard_map/all_to_all | solution.py:28
  135.7 9.1 %all-to-all-start.5 = ((bf16[4,64,160]{2,1,0:T(8,128)(2,1)}), bf16[4,64,160]{2,1,0:T(8,128)(2,1)S(1)}, u32[]{:S(2)}, u32[]{:S(2)}) async-start(bf16[4,64,160]{2,1,0:T(8,128)(2,1)} %bitcast.16), calls=%async_computation.5 | async-start | bytes 262144 | tf_op jit(solution)/shard_map/all_to_all | solution.py:299
  144.8 0.1 fusion.13
  144.9 0.8 multiply_reduce_fusion
  145.7 0.8 fusion
  146.5 0.0 copy-start.2
  146.5 0.8 fusion.9
  147.3 1.4 all-to-all-done.5
  148.8 35.4 %all_to_all.42 = bf16[32,16,128]{2,1,0:T(8,128)(2,1)S(1)} all-to-all(bf16[32,16,128]{2,1,0:T(8,128)(2,1)S(1)} %bitcast.69), channel_id=1, replica_groups=mesh['pairs'=1,'member'=2,'x'=4,'core'=2,'sp'=32] {'sp'}, dimensions={0} | all-to-all | bytes 262144 | tf_op jit(solution)/shard_map/all_to_all | solution.py:76
  184.2 1.1 broadcast_in_dim.16
  185.3 3.8 %all-to-all-start.4 = ((bf16[8,512,128]{2,1,0:T(8,128)(2,1)}), bf16[8,512,128]{2,1,0:T(8,128)(2,1)S(1)}, u32[]{:S(2)}, u32[]{:S(2)}) async-start(bf16[8,512,128]{2,1,0:T(8,128)(2,1)} %broadcast_in_dim.16), calls=%async_computation.4 | async-start | bytes 2097152 | tf_op jit(solution)/shard_map/all_to_all | solution.py:28
  189.1 0.0 copy-done.2
  189.1 23.0 %all-gather.2 = f32[8,4,320]{2,1,0:T(4,128)S(1)} all-gather(f32[1,4,320]{2,1,0:T(4,128)S(1)} %bitcast.74), channel_id=2, replica_groups=mesh['pairs'=1,'member'=2,'x'=4,'core'=2,'sp'=32] {'x','core'}, dimensions={0}, use_global_device_ids=true | all-gather | bytes 46080 | tf_op jit(solution)/shard_map/all_gather | solution.py:304
  212.1 0.1 slice_select_fusion.2
  212.2 0.1 reshape.60.gate_ref
  212.3 0.1 pad_add_fusion.place_ref
  212.4 0.1 copy.22
  212.5 0.1 reshape.59.residual_ref
  212.6 0.0 all-to-all-done.4.stripes_ref
  212.7 0.4 broadcast_in_dim.18.gates_ref
  213.1 7.6 %all-gather.5.cloned.1.call-done = bf16[46080,128]{1,0:T(8,128)(2,1)} async-done(((bf16[720,128]{1,0:T(8,128)(2,1)}), bf16[46080,128]{1,0:T(8,128)(2,1)}) %all-gather.5.cloned.1.call-update) | async-done | bytes 11796496 | tf_op jit(solution)/shard_map/all_gather | solution.py:48
  220.6 4.5 %project.1 = (f32[2,320,128]{2,1,0:T(8,128)S(1)}, bf16[8,336,128]{2,1,0:T(8,128)(2,1)}) custom-call(s32[2]{0:T(128)S(1)} %pad_add_fusion.place_ref, bf16[8,512,128]{2,1,0:T(8,128)(2,1)S(1)} %all-to-all-done.4.stripes_ref, bf16[32,2,720,128]{3,2,1,0:T(8,128)(2,1)} %bitcast.55, bf16[128,320]{1,0:T(8,128)(2,1)S(1)} %reshape.59.residual_ref, ...), custom_call_target="tpu_custom_call" | custom-call | tf_op jit(solution)/shard_map/project/pallas_call | solution.py:144
  225.1 4.6 %all-to-all-start.6 = ((bf16[8,336,128]{2,1,0:T(8,128)(2,1)}), bf16[8,336,128]{2,1,0:T(8,128)(2,1)S(1)}, u32[]{:S(2)}, u32[]{:S(2)}) async-start(bf16[8,336,128]{2,1,0:T(8,128)(2,1)} %get-tuple-element.10), calls=%async_computation.6 | async-start | bytes 1376256 | tf_op jit(solution)/shard_map/all_to_all | solution.py:317
  229.8 0.1 reshape.61.scales_ref
  229.9 10.5 %all-to-all-done.6.messages_ref = bf16[8,336,128]{2,1,0:T(8,128)(2,1)S(1)} async-done(((bf16[8,336,128]{2,1,0:T(8,128)(2,1)}), bf16[8,336,128]{2,1,0:T(8,128)(2,1)S(1)}, u32[]{:S(2)}, u32[]{:S(2)}) %all-to-all-start.6) | async-done | bytes 688160 | tf_op jit(solution)/shard_map/all_to_all | solution.py:317
  240.4 5.9 %feed.1 = bf16[2,8,160,128]{3,2,1,0:T(8,128)(2,1)S(1)} custom-call(s32[2]{0:T(128)S(1)} %pad_add_fusion.place_ref, bf16[8,336,128]{2,1,0:T(8,128)(2,1)S(1)} %all-to-all-done.6.messages_ref, f32[2,2560]{1,0:T(2,128)S(1)} %reshape.61.scales_ref, f32[8,320,128]{2,1,0:T(8,128)S(1)} %broadcast_in_dim.18.gates_ref, ...), custom_call_target="tpu_custom_call" | custom-call | tf_op jit(solution)/shard_map/feed/pallas_call | solution.py:258
  246.3 16.5 %all_to_all.43.shares_ref = bf16[16,160,128]{2,1,0:T(8,128)(2,1)S(1)} all-to-all(bf16[16,160,128]{2,1,0:T(8,128)(2,1)S(1)} %bitcast.54), channel_id=1, replica_groups=mesh['pairs'=1,'member'=2,'x'=4,'core'=2,'sp'=32] {'member','x','core'}, dimensions={0} | all-to-all | bytes 1310720 | tf_op jit(solution)/shard_map/all_to_all | solution.py:320
  262.7 0.9 finish.1
  (19 shorter events, 0.3 us)
Async XLA Ops:
  6.5 214.1 %all-gather.5.cloned.1.call-start = ((), (), s32[]{:S(2)}) async-start(), calls=%async_computation.8 | async-start | bytes 11980800 | tf_op jit(solution)/shard_map/all_gather | solution.py:48
  8.7 0.7 copy-start
  11.4 112.2 %copy-start.1 = (bf16[2,64,320]{2,1,0:T(8,128)(2,1)S(1)}, bf16[2,64,320]{2,1,0:T(8,128)(2,1)}, u32[]{:S(2)}) copy-start(bf16[2,64,320]{2,1,0:T(8,128)(2,1)} %param.11) | copy-start | bytes 245764
  119.6 16.1 %all-to-all-start.2 = ((bf16[4,2,512,128]{3,2,1,0:T(8,128)(2,1)}), bf16[4,2,512,128]{3,2,1,0:T(8,128)(2,1)S(1)}, u32[]{:S(2)}, u32[]{:S(2)}) async-start(bf16[4,2,512,128]{3,2,1,0:T(8,128)(2,1)} %broadcast_in_dim.15), calls=%async_computation.2 | async-start | bytes 2097152 | tf_op jit(solution)/shard_map/all_to_all | solution.py:28
  135.7 13.1 %all-to-all-start.5 = ((bf16[4,64,160]{2,1,0:T(8,128)(2,1)}), bf16[4,64,160]{2,1,0:T(8,128)(2,1)S(1)}, u32[]{:S(2)}, u32[]{:S(2)}) async-start(bf16[4,64,160]{2,1,0:T(8,128)(2,1)} %bitcast.16), calls=%async_computation.5 | async-start | bytes 262144 | tf_op jit(solution)/shard_map/all_to_all | solution.py:299
  146.5 42.6 %copy-start.2 = (f32[4,320]{1,0:T(4,128)S(1)}, f32[4,320]{1,0:T(4,128)}, u32[]{:S(2)}) copy-start(f32[4,320]{1,0:T(4,128)} %param.12) | copy-start | bytes 15364
  185.3 27.3 %all-to-all-start.4 = ((bf16[8,512,128]{2,1,0:T(8,128)(2,1)}), bf16[8,512,128]{2,1,0:T(8,128)(2,1)S(1)}, u32[]{:S(2)}, u32[]{:S(2)}) async-start(bf16[8,512,128]{2,1,0:T(8,128)(2,1)} %broadcast_in_dim.16), calls=%async_computation.4 | async-start | bytes 2097152 | tf_op jit(solution)/shard_map/all_to_all | solution.py:28
  225.1 15.2 %all-to-all-start.6 = ((bf16[8,336,128]{2,1,0:T(8,128)(2,1)}), bf16[8,336,128]{2,1,0:T(8,128)(2,1)S(1)}, u32[]{:S(2)}, u32[]{:S(2)}) async-start(bf16[8,336,128]{2,1,0:T(8,128)(2,1)} %get-tuple-element.10), calls=%async_computation.6 | async-start | bytes 1376256 | tf_op jit(solution)/shard_map/all_to_all | solution.py:317
Sparse Core Ops, SparseCore 0:
  9.6 211.0 all-gather.4

commit v8 on v7

--- a/solution.py
+++ b/solution.py
@@ -221,23 +221,24 @@
         tail = active[2 * core + 1]
         moved = jnp.where(lane < LANES // 2, 0.0, pltpu.roll(tail[:, LANES:], LANES // 2, 1))
         active[2 * core + 1] = jnp.concatenate([tail[:, :LANES], moved], axis=1)
-    active = [part.astype(jnp.bfloat16) for part in active]
+    kept = jnp.concatenate([part.astype(jnp.bfloat16) for part in active], axis=1)
     for copy in copies[2]:
         copy.wait()
     each = sp // tp_size
     low = lax.broadcasted_iota(jnp.int32, (half, rows), 1) < rows // 2
     for t in range(tp_size):
-        total = jnp.zeros((outs, rows), jnp.float32)
-        for core in range(CORES):
-            block = jnp.concatenate(
-                [
-                    downs[core, t * each : (t + 1) * each].reshape(each * depth, whole),
-                    ups[core, t * each : (t + 1) * each, :, whole:].reshape(each * depth, LANES),
-                ],
-                axis=1,
-            )
-            kept = jnp.concatenate([active[2 * core], active[2 * core + 1]], axis=1)
-            total = total + contract_last(block, kept)
+        block = jnp.concatenate(
+            [
+                part.reshape(each * depth, -1)
+                for core in range(CORES)
+                for part in (
+                    downs[core, t * each : (t + 1) * each],
+                    ups[core, t * each : (t + 1) * each, :, whole:],
+                )
+            ],
+            axis=1,
+        )
+        total = contract_last(block, kept)
         total = total * gates_ref[t]
         total = total + jnp.where(place_ref[0] == t // CORES, placed_ref[t % CORES], 0.0)
         top, bottom = total[:half], total[half:]

time: 271 us -> 271 us (level)
  no operation moved by 1% of the time
where the time goes in v8:
time: 271 us; the launch traced here: 270 us
  blocking collectives  182 us (67%)
  waiting for transfers between devices  30.8 us (11%)
  starting transfers between devices  21.6 us (8%)
  between operations  13.7 us (5%)
  Pallas kernels  11.2 us (4%)
  local copies, waits for them, and re-layouts  6.98 us (3%)
  other arithmetic  3.04 us (1%)
    all_to_all x1, blocking collectives, attend(): lax.all_to_all(to_heads, 'sp', split_axis=0, concat_axis=0, tiled=True)  61.6 us
    all_to_all x1, blocking collectives, attend(): lax.all_to_all(both, 'core', split_axis=0, concat_axis=0, tiled=True)  45.1 us
    all_to_all x1, blocking collectives, attend(): return lax.all_to_all(back, 'sp', split_axis=0, concat_axis=0, tiled=True)  35.4 us
    all_gather x1, blocking collectives, body(): rows_of_modulation = lax.all_gather(modulation, tp, axis=0, tiled=False)  23 us
    all_to_all x1, blocking collectives, body(): shares = lax.all_to_all(shares, ('member', 'x', 'core'), 0, 0, tiled=True)  16.5 us
    all_to_all x2, waiting for transfers between devices, sent_to_all(): return lax.all_to_all(copies, axis, split_axis=0, concat_axis=0, tiled=True)  11.2 us
    all_to_all x1, waiting for transfers between devices, body(): messages = lax.all_to_all(messages, ('member', 'x'), 0, 0, tiled=True)  10.5 us
    all_to_all x1, starting transfers between devices, body(): lax.all_to_all(parts.reshape(PAIR * batches, rows_block, half), ('member'...  9.14 us
  transfers between devices with their start and end apart: 5, of which 4 were waited for; matrix products, arithmetic and copies ran while one was open for 3% of the time, Pallas kernels for 0%

profile of v8, /device:TPU:33, one launch (start us, length us, event | category | flops | bytes accessed | tf_op | source)
XLA Modules:
  0.0 270.5 jit_solution(4037812389217675818)
XLA Ops:
  6.5 0.0 all-gather.5.cloned.1.call-start
  6.6 0.8 select_dynamic-update-slice_fusion
  7.4 1.1 slice_select_fusion
  8.6 0.1 maximum_dynamic-update-slice_fusion
  8.7 0.0 copy-start
  8.7 0.7 copy-done
  9.4 0.1 all-gather.5.cloned.1.call-update
  9.5 0.9 copy.35
  10.4 1.0 copy_bitcast_fusion
  11.4 0.0 copy-start.1
  11.5 45.1 %all_to_all.40 = bf16[2,32,3,8,128]{4,1,3,2,0:T(8,128)(2,1)S(1)} all-to-all(bf16[2,32,3,8,128]{4,1,3,2,0:T(8,128)(2,1)S(1)} %copy.18), channel_id=1, replica_groups=mesh['pairs'=1,'member'=2,'x'=4,'core'=2,'sp'=32] {'core'}, dimensions={0} | all-to-all | bytes 786432 | tf_op jit(solution)/shard_map/all_to_all | solution.py:58
  56.6 0.2 copy.19
  56.8 61.6 %all_to_all.41 = bf16[32,48,128]{2,1,0:T(8,128)(2,1)S(1)} all-to-all(bf16[32,48,128]{2,1,0:T(8,128)(2,1)S(1)} %bitcast.60), channel_id=1, replica_groups=mesh['pairs'=1,'member'=2,'x'=4,'core'=2,'sp'=32] {'sp'}, dimensions={0} | all-to-all | bytes 786432 | tf_op jit(solution)/shard_map/all_to_all | solution.py:60
  118.4 1.2 broadcast_in_dim.15
  119.6 4.0 %all-to-all-start.2 = ((bf16[4,2,512,128]{3,2,1,0:T(8,128)(2,1)}), bf16[4,2,512,128]{3,2,1,0:T(8,128)(2,1)S(1)}, u32[]{:S(2)}, u32[]{:S(2)}) async-start(bf16[4,2,512,128]{3,2,1,0:T(8,128)(2,1)} %broadcast_in_dim.15), calls=%async_computation.2 | async-start | bytes 2097152 | tf_op jit(solution)/shard_map/all_to_all | solution.py:28
  123.6 0.0 copy-done.1
  123.6 0.1 reshape.56
  123.7 0.7 copy.21
  124.4 11.2 %all-to-all-done.2 = bf16[4,2,512,128]{3,2,1,0:T(8,128)(2,1)S(1)} async-done(((bf16[4,2,512,128]{3,2,1,0:T(8,128)(2,1)}), bf16[4,2,512,128]{3,2,1,0:T(8,128)(2,1)S(1)}, u32[]{:S(2)}, u32[]{:S(2)}) %all-to-all-start.2) | async-done | bytes 1048608 | tf_op jit(solution)/shard_map/all_to_all | solution.py:28
  135.7 9.1 %all-to-all-start.5 = ((bf16[4,64,160]{2,1,0:T(8,128)(2,1)}), bf16[4,64,160]{2,1,0:T(8,128)(2,1)S(1)}, u32[]{:S(2)}, u32[]{:S(2)}) async-start(bf16[4,64,160]{2,1,0:T(8,128)(2,1)} %bitcast.16), calls=%async_computation.5 | async-start | bytes 262144 | tf_op jit(solution)/shard_map/all_to_all | solution.py:300
  144.8 0.1 fusion.13
  144.9 0.8 multiply_reduce_fusion
  145.7 0.8 fusion
  146.5 0.0 copy-start.2
  146.5 0.8 fusion.9
  147.3 1.4 all-to-all-done.5
  148.8 35.4 %all_to_all.42 = bf16[32,16,128]{2,1,0:T(8,128)(2,1)S(1)} all-to-all(bf16[32,16,128]{2,1,0:T(8,128)(2,1)S(1)} %bitcast.69), channel_id=1, replica_groups=mesh['pairs'=1,'member'=2,'x'=4,'core'=2,'sp'=32] {'sp'}, dimensions={0} | all-to-all | bytes 262144 | tf_op jit(solution)/shard_map/all_to_all | solution.py:76
  184.2 1.1 broadcast_in_dim.16
  185.3 3.8 %all-to-all-start.4 = ((bf16[8,512,128]{2,1,0:T(8,128)(2,1)}), bf16[8,512,128]{2,1,0:T(8,128)(2,1)S(1)}, u32[]{:S(2)}, u32[]{:S(2)}) async-start(bf16[8,512,128]{2,1,0:T(8,128)(2,1)} %broadcast_in_dim.16), calls=%async_computation.4 | async-start | bytes 2097152 | tf_op jit(solution)/shard_map/all_to_all | solution.py:28
  189.1 0.0 copy-done.2
  189.1 23.0 %all-gather.2 = f32[8,4,320]{2,1,0:T(4,128)S(1)} all-gather(f32[1,4,320]{2,1,0:T(4,128)S(1)} %bitcast.74), channel_id=2, replica_groups=mesh['pairs'=1,'member'=2,'x'=4,'core'=2,'sp'=32] {'x','core'}, dimensions={0}, use_global_device_ids=true | all-gather | bytes 46080 | tf_op jit(solution)/shard_map/all_gather | solution.py:305
  212.1 0.1 slice_select_fusion.2
  212.2 0.1 reshape.60.gate_ref
  212.3 0.1 pad_add_fusion.place_ref
  212.4 0.1 copy.22
  212.5 0.1 reshape.59.residual_ref
  212.6 0.0 all-to-all-done.4.stripes_ref
  212.7 0.4 broadcast_in_dim.18.gates_ref
  213.1 7.6 %all-gather.5.cloned.1.call-done = bf16[46080,128]{1,0:T(8,128)(2,1)} async-done(((bf16[720,128]{1,0:T(8,128)(2,1)}), bf16[46080,128]{1,0:T(8,128)(2,1)}) %all-gather.5.cloned.1.call-update) | async-done | bytes 11796496 | tf_op jit(solution)/shard_map/all_gather | solution.py:48
  220.6 4.5 %project.1 = (f32[2,320,128]{2,1,0:T(8,128)S(1)}, bf16[8,336,128]{2,1,0:T(8,128)(2,1)}) custom-call(s32[2]{0:T(128)S(1)} %pad_add_fusion.place_ref, bf16[8,512,128]{2,1,0:T(8,128)(2,1)S(1)} %all-to-all-done.4.stripes_ref, bf16[32,2,720,128]{3,2,1,0:T(8,128)(2,1)} %bitcast.55, bf16[128,320]{1,0:T(8,128)(2,1)S(1)} %reshape.59.residual_ref, ...), custom_call_target="tpu_custom_call" | custom-call | tf_op jit(solution)/shard_map/project/pallas_call | solution.py:144
  225.1 4.6 %all-to-all-start.6 = ((bf16[8,336,128]{2,1,0:T(8,128)(2,1)}), bf16[8,336,128]{2,1,0:T(8,128)(2,1)S(1)}, u32[]{:S(2)}, u32[]{:S(2)}) async-start(bf16[8,336,128]{2,1,0:T(8,128)(2,1)} %get-tuple-element.10), calls=%async_computation.6 | async-start | bytes 1376256 | tf_op jit(solution)/shard_map/all_to_all | solution.py:318
  229.8 0.1 reshape.61.scales_ref
  229.9 10.5 %all-to-all-done.6.messages_ref = bf16[8,336,128]{2,1,0:T(8,128)(2,1)S(1)} async-done(((bf16[8,336,128]{2,1,0:T(8,128)(2,1)}), bf16[8,336,128]{2,1,0:T(8,128)(2,1)S(1)}, u32[]{:S(2)}, u32[]{:S(2)}) %all-to-all-start.6) | async-done | bytes 688160 | tf_op jit(solution)/shard_map/all_to_all | solution.py:318
  240.4 5.9 %feed.1 = bf16[2,8,160,128]{3,2,1,0:T(8,128)(2,1)S(1)} custom-call(s32[2]{0:T(128)S(1)} %pad_add_fusion.place_ref, bf16[8,336,128]{2,1,0:T(8,128)(2,1)S(1)} %all-to-all-done.6.messages_ref, f32[2,2560]{1,0:T(2,128)S(1)} %reshape.61.scales_ref, f32[8,320,128]{2,1,0:T(8,128)S(1)} %broadcast_in_dim.18.gates_ref, ...), custom_call_target="tpu_custom_call" | custom-call | tf_op jit(solution)/shard_map/feed/pallas_call | solution.py:259
  246.3 16.5 %all_to_all.43.shares_ref = bf16[16,160,128]{2,1,0:T(8,128)(2,1)S(1)} all-to-all(bf16[16,160,128]{2,1,0:T(8,128)(2,1)S(1)} %bitcast.54), channel_id=1, replica_groups=mesh['pairs'=1,'member'=2,'x'=4,'core'=2,'sp'=32] {'member','x','core'}, dimensions={0} | all-to-all | bytes 1310720 | tf_op jit(solution)/shard_map/all_to_all | solution.py:321
  262.7 0.9 finish.1
  (19 shorter events, 0.3 us)
Async XLA Ops:
  6.5 214.1 %all-gather.5.cloned.1.call-start = ((), (), s32[]{:S(2)}) async-start(), calls=%async_computation.8 | async-start | bytes 11980800 | tf_op jit(solution)/shard_map/all_gather | solution.py:48
  8.7 0.7 copy-start
  11.4 112.2 %copy-start.1 = (bf16[2,64,320]{2,1,0:T(8,128)(2,1)S(1)}, bf16[2,64,320]{2,1,0:T(8,128)(2,1)}, u32[]{:S(2)}) copy-start(bf16[2,64,320]{2,1,0:T(8,128)(2,1)} %param.11) | copy-start | bytes 245764
  119.6 16.1 %all-to-all-start.2 = ((bf16[4,2,512,128]{3,2,1,0:T(8,128)(2,1)}), bf16[4,2,512,128]{3,2,1,0:T(8,128)(2,1)S(1)}, u32[]{:S(2)}, u32[]{:S(2)}) async-start(bf16[4,2,512,128]{3,2,1,0:T(8,128)(2,1)} %broadcast_in_dim.15), calls=%async_computation.2 | async-start | bytes 2097152 | tf_op jit(solution)/shard_map/all_to_all | solution.py:28
  135.7 13.1 %all-to-all-start.5 = ((bf16[4,64,160]{2,1,0:T(8,128)(2,1)}), bf16[4,64,160]{2,1,0:T(8,128)(2,1)S(1)}, u32[]{:S(2)}, u32[]{:S(2)}) async-start(bf16[4,64,160]{2,1,0:T(8,128)(2,1)} %bitcast.16), calls=%async_computation.5 | async-start | bytes 262144 | tf_op jit(solution)/shard_map/all_to_all | solution.py:300
  146.5 42.6 %copy-start.2 = (f32[4,320]{1,0:T(4,128)S(1)}, f32[4,320]{1,0:T(4,128)}, u32[]{:S(2)}) copy-start(f32[4,320]{1,0:T(4,128)} %param.12) | copy-start | bytes 15364
  185.3 27.3 %all-to-all-start.4 = ((bf16[8,512,128]{2,1,0:T(8,128)(2,1)}), bf16[8,512,128]{2,1,0:T(8,128)(2,1)S(1)}, u32[]{:S(2)}, u32[]{:S(2)}) async-start(bf16[8,512,128]{2,1,0:T(8,128)(2,1)} %broadcast_in_dim.16), calls=%async_computation.4 | async-start | bytes 2097152 | tf_op jit(solution)/shard_map/all_to_all | solution.py:28
  225.1 15.2 %all-to-all-start.6 = ((bf16[8,336,128]{2,1,0:T(8,128)(2,1)}), bf16[8,336,128]{2,1,0:T(8,128)(2,1)S(1)}, u32[]{:S(2)}, u32[]{:S(2)}) async-start(bf16[8,336,128]{2,1,0:T(8,128)(2,1)} %get-tuple-element.10), calls=%async_computation.6 | async-start | bytes 1376256 | tf_op jit(solution)/shard_map/all_to_all | solution.py:318
Sparse Core Ops, SparseCore 0:
  9.6 211.0 all-gather.4
